TPU v7x, 16 devices: a whole 2x2x2 slice. The times are simulated.
16 devices in a mesh: vp: 16 (over z, y, x, core).
Axes of the slice: x: 2, y: 2, z: 2, core: 2. Of those that a mesh axis runs over, the one named last changes fastest.
Arguments:
- table_in: float32 [32000, 2048], P('vp')
- table_out: float32 [32000, 2048], P('vp')
- center_ids: int32 [32768], P('vp')
- context_ids: int32 [32768], P('vp')
- negative_ids: int32 [16384], P('vp')
Outputs:
- output 1: float32 [32000, 2048], P('vp')
- output 2: float32 [32000, 2048], P('vp')
All inputs are finite; a program needn't handle non-finite values.
Results may differ from a plain program's by a relative error of at most 0.001.
Values sent between devices are 32-bit elements.
A program may use at most 1 GiB of HBM per device.

v0:
```python
import functools

import jax
import jax.numpy as jnp
from jax import lax
from jax.experimental import pallas as pl
from jax.experimental.pallas import tpu as pltpu
from jax.sharding import PartitionSpec as P

LEARN_RATE = 1.0
NEG_WEIGHT = 5.0
AXIS_NAME = 'vp'
TILE = 8
LANES = 128
SLOT_BLOCKS = 16
HEADER = 8


def up8(count):
    return (count + 7) // 8 * 8


def distinct_bound(num_ids, shards):
    common_slots = 3 * num_ids // shards
    return common_slots // 4 + (num_ids - common_slots + shards - 1) // shards


def onehot(values, size):
    return (values[:, None] == lax.broadcasted_iota(jnp.int32, (1, size), 1)).astype(jnp.bfloat16)


def dot_f32(a, b, dims):
    return lax.dot_general(a, b, (dims, ((), ())), preferred_element_type=jnp.float32)


def request_layout(id_list, shard_rows, shards, capacity):
    hot = id_list < shards * TILE
    owner = jnp.where(hot, id_list // TILE, id_list // shard_rows)
    slot = jnp.where(hot, id_list % TILE, id_list % shard_rows + TILE)
    high = onehot(owner * SLOT_BLOCKS + slot // LANES, shards * SLOT_BLOCKS)
    low = onehot(slot % LANES, LANES)
    count = dot_f32(high, low, ((0,), (0,)))
    shape = (shards * SLOT_BLOCKS, LANES)
    row_idx = lax.broadcasted_iota(jnp.int32, shape, 0)
    lane_idx = lax.broadcasted_iota(jnp.int32, shape, 1)
    lent = (row_idx % SLOT_BLOCKS == 0) & (lane_idx < TILE)
    present = (count > 0.0) | lent
    ones = present.astype(jnp.bfloat16)
    upper = (lax.broadcasted_iota(jnp.int32, (LANES, LANES), 0) <= lax.broadcasted_iota(jnp.int32, (LANES, LANES), 1)).astype(jnp.bfloat16)
    inclusive = dot_f32(ones, upper, ((1,), (0,)))
    block_total = jnp.sum(present.astype(jnp.float32), axis=1).reshape(shards, SLOT_BLOCKS)
    before = (lax.broadcasted_iota(jnp.int32, (SLOT_BLOCKS, SLOT_BLOCKS), 0) < lax.broadcasted_iota(jnp.int32, (SLOT_BLOCKS, SLOT_BLOCKS), 1))
    block_start = dot_f32(block_total.astype(jnp.bfloat16), before.astype(jnp.bfloat16), ((1,), (0,)))
    rank = inclusive - ones.astype(jnp.float32) + block_start.reshape(-1)[:, None]
    largest = jnp.max(jnp.sum(block_total, axis=1)).astype(jnp.int32)
    rank_of_id = jnp.sum(dot_f32(high, rank.astype(jnp.bfloat16), ((1,), (0,))) * low.astype(jnp.float32), axis=1).astype(jnp.int32)
    rank_or_none = jnp.where(present, rank, -1.0).reshape(shards, 1, SLOT_BLOCKS * LANES)
    cells = lax.broadcasted_iota(jnp.int32, (1, capacity, 1), 1).astype(jnp.float32)
    slots = lax.broadcasted_iota(jnp.int32, (1, 1, SLOT_BLOCKS * LANES), 2).astype(jnp.float32)
    slot_of_cell = jnp.sum(jnp.where(rank_or_none == cells, slots + 1.0, 0.0), axis=2).astype(jnp.int32) - 1
    return owner, rank_of_id, slot_of_cell, largest


def exchange(blocks):
    return lax.all_to_all(blocks, AXIS_NAME, 0, 0)


def take_rows(rows, idx):
    return rows.at[idx].get(mode='promise_in_bounds')


def meet(me, shards):
    barrier = pltpu.get_barrier_semaphore()
    for step in range(1, shards):
        pl.semaphore_signal(barrier, inc=1, device_id=(lax.rem(me + step, shards),), device_id_type=pl.DeviceIdType.MESH)
    pl.semaphore_wait(barrier, shards - 1)


def remote(src, dst, send_sem, recv_sem, peer):
    return pltpu.make_async_remote_copy(src_ref=src, dst_ref=dst, send_sem=send_sem, recv_sem=recv_sem, device_id=(peer,), device_id_type=pl.DeviceIdType.MESH)


def ask_kernel(shards, ask, in_shard, out_shard, got, lent_in, lent_out, ask_send, ask_recv, lend_send, lend_recv, own_sem):
    me = lax.axis_index(AXIS_NAME)
    meet(me, shards)

    def lend(peer, part):
        table, lent = ((in_shard, lent_in), (out_shard, lent_out))[part]
        return remote(table.at[pl.ds(pl.multiple_of(peer * TILE, TILE), TILE)], lent, lend_send.at[part, peer], lend_recv.at[part], peer)

    @pl.when(me == 0)
    def _():
        for peer in range(1, shards):
            lend(peer, 0).start()
            lend(peer, 1).start()
        pltpu.make_async_copy(in_shard.at[pl.ds(0, TILE)], lent_in, own_sem.at[0]).start()
        pltpu.make_async_copy(out_shard.at[pl.ds(0, TILE)], lent_out, own_sem.at[1]).start()

    copies = []
    for step in range(1, shards):
        peer = lax.rem(me + step, shards)
        copies.append(remote(ask.at[peer], got.at[me], ask_send.at[step], ask_recv.at[step], peer))
        copies[-1].start()
    got[me] = ask[me]
    for copy in copies:
        copy.wait()

    @pl.when(me == 0)
    def _():
        for peer in range(1, shards):
            lend(peer, 0).wait_send()
            lend(peer, 1).wait_send()
        pltpu.make_async_copy(in_shard.at[pl.ds(0, TILE)], lent_in, own_sem.at[0]).wait()
        pltpu.make_async_copy(out_shard.at[pl.ds(0, TILE)], lent_out, own_sem.at[1]).wait()

    @pl.when(me != 0)
    def _():
        lend(me, 0).wait_recv()
        lend(me, 1).wait_recv()


def ask_owners(ask, in_shard, out_shard, shards):
    depth = in_shard.shape[1]
    any_space, vmem = pl.BlockSpec(memory_space=pl.ANY), pl.BlockSpec(memory_space=pltpu.VMEM)
    tile = jax.ShapeDtypeStruct((TILE, depth), jnp.float32)
    return pl.pallas_call(
        functools.partial(ask_kernel, shards),
        out_shape=(jax.ShapeDtypeStruct(ask.shape, jnp.int32), tile, tile),
        in_specs=[vmem, any_space, any_space],
        out_specs=(vmem, vmem, vmem),
        scratch_shapes=[pltpu.SemaphoreType.DMA((shards,)), pltpu.SemaphoreType.DMA((shards,)), pltpu.SemaphoreType.DMA((2, shards)), pltpu.SemaphoreType.DMA((2,)), pltpu.SemaphoreType.DMA((2,))],
        compiler_params=pltpu.CompilerParams(collective_id=0, has_side_effects=True),
        name='ask_owners',
    )(ask, in_shard, out_shard)


def collect_kernel(shards, mine, got, send_sem, recv_sem):
    me = lax.axis_index(AXIS_NAME)
    ready = pltpu.get_barrier_semaphore()

    @pl.when(me == 0)
    def _():
        for peer in range(1, shards):
            pl.semaphore_signal(ready, inc=1, device_id=(peer,), device_id_type=pl.DeviceIdType.MESH)
        got[0] = mine[...]
        for peer in range(1, shards):
            remote(mine, got.at[peer], send_sem, recv_sem.at[peer], 0).wait_recv()

    @pl.when(me != 0)
    def _():
        pl.semaphore_wait(ready, 1)
        got[...] = jnp.zeros_like(got)
        copy = remote(mine, got.at[me], send_sem, recv_sem.at[me], 0)
        copy.start()
        copy.wait_send()


def collect_lent(mine, shards):
    vmem = pl.BlockSpec(memory_space=pltpu.VMEM)
    got = pl.pallas_call(
        functools.partial(collect_kernel, shards),
        out_shape=jax.ShapeDtypeStruct((shards,) + mine.shape, jnp.float32),
        in_specs=[vmem],
        out_specs=vmem,
        scratch_shapes=[pltpu.SemaphoreType.DMA, pltpu.SemaphoreType.DMA((shards,))],
        compiler_params=pltpu.CompilerParams(collective_id=1, has_side_effects=True),
        name='collect_lent',
    )(mine)
    return got.reshape(-1, mine.shape[1])


GROUP = 4
BUFFERS = 4


def apply_kernel(shards, caps, num_rows, *refs):
    lists = len(caps)
    rows, (lent, table), grads, out = refs[:lists], refs[lists:lists + 2], refs[lists + 2:2 * lists + 2], refs[2 * lists + 2]
    total, buf, load_sem, grad_sem, store_sem = refs[2 * lists + 3:]
    load = pltpu.make_async_copy(table, total.at[pl.ds(0, num_rows)], load_sem)
    load.start()

    def copy(i, source):
        place = lax.rem(source, BUFFERS)
        return pltpu.make_async_copy(grads[i].at[source], buf.at[place, pl.ds(0, caps[i])], grad_sem.at[place])

    for i in range(lists):
        for source in range(BUFFERS - 1):
            copy(i, source).start()
        if i == 0:
            load.wait()
            total[pl.ds(0, lent.shape[0]), :] += lent[...]

        def from_source(source, carry):
            @pl.when(source + BUFFERS - 1 < shards)
            def _():
                copy(i, source + BUFFERS - 1).start()

            copy(i, source).wait()
            place = lax.rem(source, BUFFERS)

            def group(number, carry):
                base = source * caps[i] + number * GROUP
                idx = [rows[i][base + k] for k in range(GROUP)]
                sums = [total[pl.ds(idx[k], 1), :] + buf[place, pl.ds(number * GROUP + k, 1), :] for k in range(GROUP)]
                for k in range(GROUP):
                    total[pl.ds(idx[k], 1), :] = sums[k]
                return carry

            return lax.fori_loop(TILE // GROUP, caps[i] // GROUP, group, carry)

        lax.fori_loop(0, shards, from_source, 0)
    store = pltpu.make_async_copy(total.at[pl.ds(0, num_rows)], out, store_sem)
    store.start()
    store.wait()


def apply_rows(table, lent, slots, grads):
    num_rows, depth = table.shape
    shards = grads[0].shape[0]
    caps = tuple(g.shape[1] for g in grads)
    rows = [jnp.where(slot < TILE, num_rows, slot - TILE).reshape(-1) for slot in slots]
    any_space = pl.BlockSpec(memory_space=pl.ANY)
    moved = 2 * num_rows + sum(caps) * shards
    return pl.pallas_call(
        functools.partial(apply_kernel, shards, caps, num_rows),
        out_shape=jax.ShapeDtypeStruct(table.shape, jnp.float32),
        in_specs=[pl.BlockSpec(memory_space=pltpu.SMEM)] * len(caps) + [pl.BlockSpec(memory_space=pltpu.VMEM), any_space] + [any_space] * len(caps),
        out_specs=any_space,
        scratch_shapes=[pltpu.VMEM((num_rows + TILE, depth), jnp.float32), pltpu.VMEM((BUFFERS, max(caps), depth), jnp.float32), pltpu.SemaphoreType.DMA, pltpu.SemaphoreType.DMA((BUFFERS,)), pltpu.SemaphoreType.DMA],
        compiler_params=pltpu.CompilerParams(vmem_limit_bytes=40 * 2**20),
        cost_estimate=pl.CostEstimate(flops=40 * moved * depth, bytes_accessed=4 * moved * depth, transcendentals=0),
        name='apply_rows',
    )(*rows, lent, table, *grads)


def solution(mesh):
    shards = mesh.shape[AXIS_NAME]

    def device_step(in_shard, out_shard, center_ids, context_ids, negative_ids):
        shard_rows, depth = in_shard.shape
        num_negs = negative_ids.shape[0]
        lists = (center_ids, context_ids, negative_ids)
        full = tuple(up8(distinct_bound(ids.shape[0], shards) + TILE) for ids in lists)
        usual = tuple(up8(TILE + ids.shape[0] * 13 // (16 * shards)) for ids in lists)

        owners, ranks, asks, largest = zip(*(request_layout(ids, shard_rows, shards, cap) for ids, cap in zip(lists, full)))
        counts = jnp.broadcast_to(jnp.stack(largest)[None, :], (shards, 3))
        ask = jnp.concatenate(asks + (counts,), axis=1)
        ask = jnp.pad(ask, ((0, 0), (0, HEADER * LANES - ask.shape[1]))).reshape(shards, HEADER, LANES)
        arrived, lent_in, lent_out = ask_owners(ask, in_shard, out_shard, shards)
        arrived = arrived.reshape(shards, HEADER * LANES)
        edge1, edge2, edge3 = full[0], full[0] + full[1], sum(full)
        slots = (arrived[:, :edge1], arrived[:, edge1:edge2], arrived[:, edge2:edge3])
        most = jnp.max(arrived[:, edge3:edge3 + 3], axis=0)
        unit = jnp.where(most[2] >= 0, 1.0, 0.0)
        fits = jnp.all(most <= jnp.array(usual, jnp.int32))

        def run(caps, in_shard, out_shard, lent_in, lent_out, owners, ranks, slots, unit):
            cell_of_id = [owner * cap + rank for owner, rank, cap in zip(owners, ranks, caps)]
            asked = [slot[:, :cap] for slot, cap in zip(slots, caps)]

            def pick(table, lent, slot):
                rows = take_rows(table, jnp.maximum(slot - TILE, 0))
                return lax.dynamic_update_slice(rows, jnp.broadcast_to(lent[None], (shards, TILE, depth)), (0, 0, 0))

            def fetch(rows):
                return exchange(rows).reshape(-1, depth)

            def send_back(grads, cells, cap):
                summed = jnp.zeros((shards * cap, depth), jnp.float32).at[cells].add(grads, mode='promise_in_bounds')
                return exchange(summed.reshape(shards, cap, depth))

            picked_neg, slot_in, slot_ctx = lax.optimization_barrier((pick(out_shard, lent_out, asked[2]), asked[0], asked[1]))
            neg_rows = fetch(picked_neg)
            picked_in, slot_ctx = lax.optimization_barrier((pick(in_shard, lent_in, slot_in), slot_ctx))
            in_rows = fetch(picked_in)
            ctx_rows = fetch(pick(out_shard, lent_out, slot_ctx))

            negative_half = (take_rows(neg_rows, cell_of_id[2]) * unit).astype(jnp.bfloat16)
            center_vec = take_rows(in_rows, cell_of_id[0])
            center_half = center_vec.astype(jnp.bfloat16)
            neg_score = dot_f32(center_half, negative_half, ((1,), (1,)))
            neg_grad = ((NEG_WEIGHT / num_negs) * jax.nn.sigmoid(neg_score)).astype(jnp.bfloat16)
            d_negative = -dot_f32(neg_grad, center_half, ((0,), (0,)))
            neg_back = send_back(d_negative, cell_of_id[2], caps[2])
            d_center_neg = dot_f32(neg_grad, negative_half, ((1,), (0,)))

            context_vec = take_rows(ctx_rows, cell_of_id[1])
            pos_grad = (jax.nn.sigmoid(jnp.sum(center_vec * context_vec, axis=1)) - 1.0)[:, None]
            ctx_back = send_back(-(pos_grad * center_vec), cell_of_id[1], caps[1])
            in_back = send_back(-(pos_grad * context_vec + d_center_neg), cell_of_id[0], caps[0])

            lent_sum = LEARN_RATE * (jnp.sum(neg_back[:, :TILE], axis=0) + jnp.sum(ctx_back[:, :TILE], axis=0))
            new_out = apply_rows(out_shard, collect_lent(lent_sum, shards), (asked[2], asked[1]), (neg_back, ctx_back))
            lent_sum = LEARN_RATE * jnp.sum(in_back[:, :TILE], axis=0)
            new_in = apply_rows(in_shard, collect_lent(lent_sum, shards), (asked[0],), (in_back,))
            return new_in, new_out

        def branch(caps):
            def call(*args):
                return run(caps, *args)

            return call

        args = (in_shard, out_shard, lent_in, lent_out, owners, ranks, slots, unit)
        return lax.cond(fits, branch(usual), branch(full), *args)

    return jax.shard_map(device_step, mesh=mesh, in_specs=(P(AXIS_NAME, None), P(AXIS_NAME, None), P(AXIS_NAME), P(AXIS_NAME), P(AXIS_NAME)), out_specs=(P(AXIS_NAME, None), P(AXIS_NAME, None)), check_vma=False)
```

profile of v0, /device:TPU:0, one launch (start us, length us, event | category | flops | bytes accessed | tf_op | source)
XLA Modules:
  0.0 1079.5 jit_solution(4044427375262059003)
XLA Ops:
  8.1 5.5 select_reduce_fusion.1
  18.6 20.2 %ask_owners.1 = (s32[16,8,128]{2,1,0:T(8,128)}, f32[8,2048]{1,0:T(8,128)S(1)}, f32[8,2048]{1,0:T(8,128)S(1)}) custom-call(s32[16,8,128]{2,1,0:T(8,128)} %bitcast.69, f32[2000,2048]{1,0:T(8,128)} %in_shard.1, f32[2000,2048]{1,0:T(8,128)} %out_shard.1), custom_call_target="tpu_custom_call" | custom-call | tf_op jit(solution)/shard_map/ask_owners/pallas_call | solution.py:126
  43.4 1034.6 %conditional.1 = (f32[2000,2048]{1,0:T(8,128)}, f32[2000,2048]{1,0:T(8,128)}) conditional(s32[]{:T(128)} %convert_element_type.174, (s32[16,1024]{1,0:T(8,128)S(1)}, s32[2048]{0:T(1024)S(1)}, s32[2048]{0:T(1024)S(1)}, s32[16,1024]{1,0:T(8,128)S(1)}, f32[2000,2048]{1,0:T(8,128)}, /*index=5*/f32[8,2048]{1,0:T(8,128)S(1)}, s32[16,1024]{1,0:T(8,128)S(1)}, ...), branch_computations={%region_17.25_spmd, %region_25.33_spmd} | conditional | flops 27187271680 | bytes 1197955200 | solution.py:307
  49.5 14.5 %gather_fusion.6 = f32[1024,2048]{1,0:T(8,128)} fusion(f32[2000,2048]{1,0:T(8,128)} %get-tuple-element.79.refs_3_, s32[1024]{0:T(1024)S(1)} %broadcast_clamp_fusion.6), kind=kCustom, calls=%fused_computation.6 | custom fusion | bytes 16781312 | tf_op jit(solution)/shard_map/cond/branch_1_fun/gather | solution.py:69
  65.1 4.3 all-to-all-start.8
  69.5 20.0 %gather_fusion.7 = f32[1792,2048]{1,0:T(8,128)} fusion(f32[2000,2048]{1,0:T(8,128)} %get-tuple-element.78.refs_2_, s32[2048]{0:T(1024)S(1)} %pad_clamp_fusion.4), kind=kCustom, calls=%fused_computation.7 | custom fusion | bytes 29367296 | tf_op jit(solution)/shard_map/cond/branch_1_fun/gather | solution.py:69
  90.6 80.4 %all-to-all-done.8 = f32[16,64,2048]{2,1,0:T(8,128)} async-done(((f32[16,64,2048]{2,1,0:T(8,128)}), f32[16,64,2048]{2,1,0:T(8,128)}, u32[]{:S(2)}, u32[]{:S(2)}) %all-to-all-start.8) | async-done | bytes 8388640 | tf_op jit(solution)/shard_map/cond/branch_1_fun/all_to_all | solution.py:65
  171.0 4.3 all-to-all-start.6
  175.4 20.0 %gather_fusion.9 = f32[1792,2048]{1,0:T(8,128)} fusion(f32[2000,2048]{1,0:T(8,128)} %get-tuple-element.79.refs_3_, s32[2048]{0:T(1024)S(1)} %pad_clamp_fusion.3), kind=kCustom, calls=%fused_computation.9 | custom fusion | bytes 29367296 | tf_op jit(solution)/shard_map/cond/branch_1_fun/gather | solution.py:69
  196.5 154.5 %all-to-all-done.6 = f32[16,112,2048]{2,1,0:T(8,128)} async-done(((f32[16,112,2048]{2,1,0:T(8,128)}), f32[16,112,2048]{2,1,0:T(8,128)}, u32[]{:S(2)}, u32[]{:S(2)}) %all-to-all-start.6) | async-done | bytes 14680096 | tf_op jit(solution)/shard_map/cond/branch_1_fun/all_to_all | solution.py:65
  351.0 4.6 all-to-all-start.7
  357.4 12.2 %gather_fusion.11 = f32[1024,2048]{1,0:T(8,128)} fusion(f32[1024,2048]{1,0:T(8,128)} %bitcast.17, s32[1024]{0:T(1024)S(1)} %get-tuple-element.134), kind=kCustom, calls=%fused_computation.11 | custom fusion | bytes 16781312 | tf_op jit(solution)/shard_map/cond/branch_1_fun/gather | solution.py:69
  369.6 21.7 %gather_fusion.8 = f32[2048,2048]{1,0:T(8,128)} fusion(f32[1792,2048]{1,0:T(8,128)} %bitcast.14, s32[2048]{0:T(1024)S(1)} %get-tuple-element.136), kind=kCustom, calls=%fused_computation.8 | custom fusion | bytes 33562624 | tf_op jit(solution)/shard_map/cond/branch_1_fun/gather | solution.py:69
  391.4 15.7 %multiply_convert_fusion.4 = bf16[2048,1024]{1,0:T(8,128)(2,1)S(1)} fusion(f32[2048,2048]{1,0:T(8,128)} %gather_fusion.8, f32[1024,2048]{1,0:T(8,128)} %gather_fusion.11, f32[]{:T(128)} %bitcast.18), kind=kOutput, calls=%fused_computation.71 | convolution fusion | flops 8608808960 | bytes 29360132 | tf_op jit(solution)/shard_map/cond/branch_1_fun/dot_general | solution.py:33
  407.1 16.4 %fusion.31 = f32[1024,2048]{1,0:T(8,128)} fusion(bf16[2048,1024]{1,0:T(8,128)(2,1)S(1)} %multiply_convert_fusion.4, f32[2048,2048]{1,0:T(8,128)} %gather_fusion.8), kind=kOutput, calls=%fused_computation.78 | convolution fusion | flops 8594128896 | bytes 29360128 | tf_op jit(solution)/shard_map/cond/branch_1_fun/dot_general | solution.py:33
  423.5 19.1 %scatter_custom_fusion.4 = f32[1024,2048]{1,0:T(8,128)} fusion(s32[1024]{0:T(1024)S(1)} %get-tuple-element.135, f32[1024,2048]{1,0:T(8,128)} %fusion.31, f32[]{:T(128)} %constant.234.clone), kind=kCustom, calls=%fused_computation.69 | custom fusion | flops 4194304 | bytes 16777220 | tf_op jit(solution)/shard_map/cond/branch_1_fun/scatter-add | solution.py:271
  442.6 88.6 %all-to-all-done.7 = f32[16,112,2048]{2,1,0:T(8,128)} async-done(((f32[16,112,2048]{2,1,0:T(8,128)}), f32[16,112,2048]{2,1,0:T(8,128)}, u32[]{:S(2)}, u32[]{:S(2)}) %all-to-all-start.7) | async-done | bytes 14680096 | tf_op jit(solution)/shard_map/cond/branch_1_fun/all_to_all | solution.py:65
  531.2 4.3 all-to-all-start.10
  535.6 21.7 %gather_fusion.10 = f32[2048,2048]{1,0:T(8,128)} fusion(f32[1792,2048]{1,0:T(8,128)} %bitcast.16, s32[2048]{0:T(1024)S(1)} %get-tuple-element.132), kind=kCustom, calls=%fused_computation.10 | custom fusion | bytes 33562624 | tf_op jit(solution)/shard_map/cond/branch_1_fun/gather | solution.py:69
  557.3 11.5 %multiply_reduce_fusion.1 = f32[2048]{0:T(1024)S(1)} fusion(f32[2048,2048]{1,0:T(8,128)} %gather_fusion.8, f32[2048,2048]{1,0:T(8,128)} %gather_fusion.10), kind=kLoop, calls=%fused_computation.68 | loop fusion | flops 8386560 | bytes 33562624 | tf_op jit(solution)/shard_map/cond/branch_1_fun/reduce_sum | solution.py:290
  569.1 14.7 %fusion.34 = f32[2048,2048]{1,0:T(8,128)} fusion(bf16[2048,1024]{1,0:T(8,128)(2,1)S(1)} %copy-done.31, f32[1024,2048]{1,0:T(8,128)} %gather_fusion.11, f32[]{:T(128)} %bitcast.18), kind=kOutput, calls=%fused_computation.81 | convolution fusion | flops 8594128896 | bytes 29360132 | tf_op jit(solution)/shard_map/cond/branch_1_fun/dot_general | solution.py:33
  583.8 37.2 %scatter_custom_fusion.3 = f32[1792,2048]{1,0:T(8,128)} fusion(s32[2048]{0:T(1024)} %get-tuple-element.137, f32[2048,2048]{1,0:T(8,128)} %fusion.34, f32[2048,2048]{1,0:T(8,128)} %gather_fusion.10, f32[2048]{0:T(1024)S(1)} %divide_add_fusion.1, f32[]{:T(128)} %constant.234.clone), kind=kCustom, calls=%fused_computation.64 | custom fusion | flops 16777216 | bytes 48243200 | tf_op jit(solution)/shard_map/cond/branch_1_fun/scatter-add | solution.py:271
  621.0 16.2 %all-to-all-done.10.refs_4_ = f32[16,64,2048]{2,1,0:T(8,128)} async-done(((f32[16,64,2048]{2,1,0:T(8,128)}), f32[16,64,2048]{2,1,0:T(8,128)}, u32[]{:S(2)}, u32[]{:S(2)}) %all-to-all-start.10) | async-done | bytes 8388640 | tf_op jit(solution)/shard_map/cond/branch_1_fun/all_to_all | solution.py:65
  637.2 4.5 all-to-all-start.9
  641.7 35.2 %scatter_custom_fusion.5 = f32[1792,2048]{1,0:T(8,128)} fusion(s32[2048]{0:T(1024)S(1)} %get-tuple-element.133, f32[2048,2048]{1,0:T(8,128)} %gather_fusion.8, f32[2048]{0:T(1024)S(1)} %divide_add_fusion.1, f32[]{:T(128)} %constant.234.clone), kind=kCustom, calls=%fused_computation.61 | custom fusion | flops 12582912 | bytes 31465476 | tf_op jit(solution)/shard_map/cond/branch_1_fun/scatter-add | solution.py:271
  676.9 140.4 %all-to-all-done.9.refs_3_ = f32[16,112,2048]{2,1,0:T(8,128)} async-done(((f32[16,112,2048]{2,1,0:T(8,128)}), f32[16,112,2048]{2,1,0:T(8,128)}, u32[]{:S(2)}, u32[]{:S(2)}) %all-to-all-start.9) | async-done | bytes 14680096 | tf_op jit(solution)/shard_map/cond/branch_1_fun/all_to_all | solution.py:65
  817.3 4.1 all-to-all-start.11
  823.0 1.9 slice_reduce_fusion.5.mine
  824.9 177.0 %collect_lent.6 = f32[16,8,2048]{2,1,0:T(8,128)} custom-call(f32[8,2048]{1,0:T(8,128)} %slice_reduce_fusion.5.mine), custom_call_target="tpu_custom_call" | custom-call | tf_op jit(solution)/shard_map/cond/branch_1_fun/collect_lent/pallas_call | solution.py:160
  1003.9 10.7 collect_lent.7
  1015.8 26.6 %apply_rows.6 = f32[2000,2048]{1,0:T(8,128)} custom-call(s32[1792]{0:T(1024)S(1)} %reshape.125.refs_0_, f32[128,2048]{1,0:T(8,128)S(1)} %bitcast.46, f32[2000,2048]{1,0:T(8,128)} %get-tuple-element.78.refs_2_, f32[16,112,2048]{2,1,0:T(8,128)} %all-to-all-done.9.refs_3_), custom_call_target="tpu_custom_call" | custom-call | flops 474480640 | bytes 47448064 | tf_op jit(solution)/shard_map/cond/branch_1_fun/apply_rows/pallas_call | solution.py:225
  1042.4 35.3 %apply_rows.7 = f32[2000,2048]{1,0:T(8,128)} custom-call(s32[1024]{0:T(1024)S(1)} %reshape.131.refs_0_, s32[1792]{0:T(1024)S(1)} %reshape.132.refs_1_, f32[128,2048]{1,0:T(8,128)S(1)} %bitcast.47, f32[2000,2048]{1,0:T(8,128)} %get-tuple-element.79.refs_3_, f32[16,64,2048]{2,1,0:T(8,128)} %all-to-all-done.10.refs_4_, f32[16,112,2048]{2,1,0:T(8,128)} %all-to-all-done.11.refs_5_), custom_call_target="tpu_custom_call" | custom-call | flops 558366720 | bytes 55836672 | tf_op jit(solution)/shard_map/cond/branch_1_fun/apply_rows/pallas_call | solution.py:225
  (98 shorter events, 25.4 us)
Async XLA Ops:
  18.6 21.1 %copy-start.27 = (s32[3]{0:T(128)S(1)}, s32[3]{0:T(128)}, u32[]{:S(2)}) copy-start(s32[3]{0:T(128)} %constant.263.clone) | copy-start | bytes 40
  65.1 105.9 %all-to-all-start.8 = ((f32[16,64,2048]{2,1,0:T(8,128)}), f32[16,64,2048]{2,1,0:T(8,128)}, u32[]{:S(2)}, u32[]{:S(2)}) async-start(f32[16,64,2048]{2,1,0:T(8,128)} %broadcast_dynamic-update-slice_fusion.5), calls=%async_computation.8 | async-start | bytes 16777216 | tf_op jit(solution)/shard_map/cond/branch_1_fun/all_to_all | solution.py:65
  171.0 180.0 %all-to-all-start.6 = ((f32[16,112,2048]{2,1,0:T(8,128)}), f32[16,112,2048]{2,1,0:T(8,128)}, u32[]{:S(2)}, u32[]{:S(2)}) async-start(f32[16,112,2048]{2,1,0:T(8,128)} %broadcast_dynamic-update-slice_fusion.3), calls=%async_computation.6 | async-start | bytes 29360128 | tf_op jit(solution)/shard_map/cond/branch_1_fun/all_to_all | solution.py:65
  351.0 180.2 %all-to-all-start.7 = ((f32[16,112,2048]{2,1,0:T(8,128)}), f32[16,112,2048]{2,1,0:T(8,128)}, u32[]{:S(2)}, u32[]{:S(2)}) async-start(f32[16,112,2048]{2,1,0:T(8,128)} %broadcast_dynamic-update-slice_fusion.4), calls=%async_computation.7 | async-start | bytes 29360128 | tf_op jit(solution)/shard_map/cond/branch_1_fun/all_to_all | solution.py:65
  407.1 16.4 %copy-start.30 = (bf16[2048,1024]{1,0:T(8,128)(2,1)}, bf16[2048,1024]{1,0:T(8,128)(2,1)S(1)}, u32[]{:S(2)}) copy-start(bf16[2048,1024]{1,0:T(8,128)(2,1)S(1)} %multiply_convert_fusion.4) | copy-start | bytes 12582916 | tf_op jit(solution)/shard_map/cond
  423.5 112.0 %copy-start.10 = (s32[2048]{0:T(1024)S(1)}, s32[2048]{0:T(1024)}, u32[]{:S(2)}) copy-start(s32[2048]{0:T(1024)} %get-tuple-element.89) | copy-start | bytes 24580 | tf_op jit(solution)/shard_map/cond
  423.5 112.0 %copy-start.14 = (s32[2048]{0:T(1024)S(1)}, s32[2048]{0:T(1024)}, u32[]{:S(2)}) copy-start(s32[2048]{0:T(1024)} %get-tuple-element.88) | copy-start | bytes 24580 | tf_op jit(solution)/shard_map/cond
  531.2 106.0 %all-to-all-start.10 = ((f32[16,64,2048]{2,1,0:T(8,128)}), f32[16,64,2048]{2,1,0:T(8,128)}, u32[]{:S(2)}, u32[]{:S(2)}) async-start(f32[16,64,2048]{2,1,0:T(8,128)} %bitcast.59), calls=%async_computation.10 | async-start | bytes 16777216 | tf_op jit(solution)/shard_map/cond/branch_1_fun/all_to_all | solution.py:65
  557.3 11.8 %copy-start.31 = (bf16[2048,1024]{1,0:T(8,128)(2,1)S(1)}, bf16[2048,1024]{1,0:T(8,128)(2,1)}, u32[]{:S(2)}) copy-start(bf16[2048,1024]{1,0:T(8,128)(2,1)} %copy-done.30) | copy-start | bytes 12582916 | tf_op jit(solution)/shard_map/cond
  637.2 180.1 %all-to-all-start.9 = ((f32[16,112,2048]{2,1,0:T(8,128)}), f32[16,112,2048]{2,1,0:T(8,128)}, u32[]{:S(2)}, u32[]{:S(2)}) async-start(f32[16,112,2048]{2,1,0:T(8,128)} %bitcast.57), calls=%async_computation.9 | async-start | bytes 29360128 | tf_op jit(solution)/shard_map/cond/branch_1_fun/all_to_all | solution.py:65
  817.3 4.2 copy-start.24
  817.3 4.2 copy-start.22
  817.3 4.3 copy-start.23
  817.3 184.6 %all-to-all-start.11 = ((f32[16,112,2048]{2,1,0:T(8,128)}), f32[16,112,2048]{2,1,0:T(8,128)}, u32[]{:S(2)}, u32[]{:S(2)}) async-start(f32[16,112,2048]{2,1,0:T(8,128)} %bitcast.56), calls=%async_computation.11 | async-start | bytes 29360128 | tf_op jit(solution)/shard_map/cond/branch_1_fun/all_to_all | solution.py:65
  1014.6 1.2 copy-start.2
  1015.8 26.6 %copy-start.3 = (f32[16,8,2048]{2,1,0:T(8,128)S(1)}, f32[16,8,2048]{2,1,0:T(8,128)}, u32[]{:S(2)}) copy-start(f32[16,8,2048]{2,1,0:T(8,128)} %collect_lent.7) | copy-start | bytes 3145732 | tf_op jit(solution)/shard_map/cond
where the time goes:
time: 1090 us; the launch traced here: 1080 us
  waiting for transfers between devices  480 us (44%)
  Pallas kernels  270 us (25%)
  other arithmetic  123 us (11%)
  local copies, waits for them, and re-layouts  118 us (11%)
  matrix products  51.4 us (5%)
  starting transfers between devices  26.2 us (2%)
    all_to_all x6, waiting for transfers between devices, exchange(): return lax.all_to_all(blocks, AXIS_NAME, 0, 0)  480 us
    pallas_call x2, Pallas kernels, collect_lent(): pl.pallas_call(functools.partial(collect_kernel, shards), out_shape=jax.S...  188 us
    gather x6, local copies, waits for them, and re-layouts, take_rows(): return rows.at[idx].get(mode='promise_in_bounds')  110 us
    scatter-add x3, other arithmetic, send_back(): jnp.zeros((shards * cap, depth), jnp.float32).at[cells]  91.5 us
    pallas_call x2, Pallas kernels, apply_rows(): pl.pallas_call(functools.partial(apply_kernel, shards, caps, num_rows), o...  61.9 us
    dot_general x15, matrix products, dot_f32(): lax.dot_general(a, b, (dims, ((), ())), preferred_element_type=jnp.float32)  51.4 us
    all_to_all x6, starting transfers between devices, exchange(): return lax.all_to_all(blocks, AXIS_NAME, 0, 0)  26.2 us
  transfers between devices with their start and end apart: 6, of which 5 were waited for; matrix products, arithmetic and copies ran while one was open for 23% of the time, Pallas kernels for 16%

commit v1 on v0

--- a/solution.py
+++ b/solution.py
@@ -134,6 +134,41 @@
     )(ask, in_shard, out_shard)
 
 
+def exchange_kernel(shards, blocks, got, send_sem, recv_sem, own_sem):
+    me = lax.axis_index(AXIS_NAME)
+    meet(me, shards)
+    own = pltpu.make_async_copy(blocks.at[me], got.at[me], own_sem)
+    own.start()
+
+    def copy(step, rows):
+        peer = lax.rem(me + step, shards)
+        return remote(blocks.at[peer, rows], got.at[me, rows], send_sem.at[step], recv_sem.at[step], peer)
+
+    def send(tile, carry):
+        for step in range(1, shards):
+            copy(step, pl.ds(pl.multiple_of(tile * TILE, TILE), TILE)).start()
+        return carry
+
+    count = blocks.shape[1]
+    lax.fori_loop(0, count // TILE, send, 0)
+    for step in range(1, shards):
+        copy(step, pl.ds(0, count)).wait()
+    own.wait()
+
+
+def exchange_rows(blocks, collective_id):
+    shards = blocks.shape[0]
+    any_space = pl.BlockSpec(memory_space=pl.ANY)
+    return pl.pallas_call(
+        functools.partial(exchange_kernel, shards),
+        out_shape=jax.ShapeDtypeStruct(blocks.shape, jnp.float32),
+        in_specs=[any_space],
+        out_specs=any_space,
+        scratch_shapes=[pltpu.SemaphoreType.DMA((shards,)), pltpu.SemaphoreType.DMA((shards,)), pltpu.SemaphoreType.DMA],
+        compiler_params=pltpu.CompilerParams(collective_id=collective_id, has_side_effects=True),
+    )(blocks)
+
+
 def collect_kernel(shards, mine, got, send_sem, recv_sem):
     me = lax.axis_index(AXIS_NAME)
     ready = pltpu.get_barrier_semaphore()
@@ -157,7 +192,7 @@
 
 def collect_lent(mine, shards):
     vmem = pl.BlockSpec(memory_space=pltpu.VMEM)
-    got = pl.pallas_call(
+    return pl.pallas_call(
         functools.partial(collect_kernel, shards),
         out_shape=jax.ShapeDtypeStruct((shards,) + mine.shape, jnp.float32),
         in_specs=[vmem],
@@ -166,53 +201,74 @@
         compiler_params=pltpu.CompilerParams(collective_id=1, has_side_effects=True),
         name='collect_lent',
     )(mine)
-    return got.reshape(-1, mine.shape[1])
 
 
 GROUP = 4
 BUFFERS = 4
+PARTS = 2
 
 
 def apply_kernel(shards, caps, num_rows, *refs):
     lists = len(caps)
     rows, (lent, table), grads, out = refs[:lists], refs[lists:lists + 2], refs[lists + 2:2 * lists + 2], refs[2 * lists + 2]
     total, buf, load_sem, grad_sem, store_sem = refs[2 * lists + 3:]
-    load = pltpu.make_async_copy(table, total.at[pl.ds(0, num_rows)], load_sem)
-    load.start()
-
-    def copy(i, source):
+    width = table.shape[1] // PARTS
+    segments = [(part, i) for part in range(PARTS) for i in range(lists)]
+
+    def columns(part):
+        return pl.ds(part * width, width)
+
+    def load(part):
+        return pltpu.make_async_copy(table.at[:, columns(part)], total.at[pl.ds(0, num_rows), columns(part)], load_sem.at[part])
+
+    def store(part):
+        return pltpu.make_async_copy(total.at[pl.ds(0, num_rows), columns(part)], out.at[:, columns(part)], store_sem.at[part])
+
+    def copy(segment, source):
+        part, i = segment
         place = lax.rem(source, BUFFERS)
-        return pltpu.make_async_copy(grads[i].at[source], buf.at[place, pl.ds(0, caps[i])], grad_sem.at[place])
-
-    for i in range(lists):
-        for source in range(BUFFERS - 1):
-            copy(i, source).start()
+        return pltpu.make_async_copy(grads[i].at[source, :, columns(part)], buf.at[place, pl.ds(0, caps[i])], grad_sem.at[place])
+
+    for part in range(PARTS):
+        load(part).start()
+    for source in range(BUFFERS - 1):
+        copy(segments[0], source).start()
+    for number, segment in enumerate(segments):
+        part, i = segment
         if i == 0:
-            load.wait()
-            total[pl.ds(0, lent.shape[0]), :] += lent[...]
+            load(part).wait()
+            total[pl.ds(0, lent.shape[0]), columns(part)] += lent[:, columns(part)]
 
         def from_source(source, carry):
-            @pl.when(source + BUFFERS - 1 < shards)
+            ahead = source + BUFFERS - 1
+
+            @pl.when(ahead < shards)
             def _():
-                copy(i, source + BUFFERS - 1).start()
-
-            copy(i, source).wait()
+                copy(segment, ahead).start()
+
+            if number + 1 < len(segments):
+                @pl.when(ahead >= shards)
+                def _():
+                    copy(segments[number + 1], ahead - shards).start()
+
+            copy(segment, source).wait()
             place = lax.rem(source, BUFFERS)
 
-            def group(number, carry):
-                base = source * caps[i] + number * GROUP
+            def group(step, carry):
+                base = source * caps[i] + step * GROUP
                 idx = [rows[i][base + k] for k in range(GROUP)]
-                sums = [total[pl.ds(idx[k], 1), :] + buf[place, pl.ds(number * GROUP + k, 1), :] for k in range(GROUP)]
+                sums = [total[pl.ds(idx[k], 1), columns(part)] + buf[place, pl.ds(step * GROUP + k, 1), :] for k in range(GROUP)]
                 for k in range(GROUP):
-                    total[pl.ds(idx[k], 1), :] = sums[k]
+                    total[pl.ds(idx[k], 1), columns(part)] = sums[k]
                 return carry
 
             return lax.fori_loop(TILE // GROUP, caps[i] // GROUP, group, carry)
 
         lax.fori_loop(0, shards, from_source, 0)
-    store = pltpu.make_async_copy(total.at[pl.ds(0, num_rows)], out, store_sem)
-    store.start()
-    store.wait()
+        if i == lists - 1:
+            store(part).start()
+    for part in range(PARTS):
+        store(part).wait()
 
 
 def apply_rows(table, lent, slots, grads):
@@ -227,7 +283,7 @@
         out_shape=jax.ShapeDtypeStruct(table.shape, jnp.float32),
         in_specs=[pl.BlockSpec(memory_space=pltpu.SMEM)] * len(caps) + [pl.BlockSpec(memory_space=pltpu.VMEM), any_space] + [any_space] * len(caps),
         out_specs=any_space,
-        scratch_shapes=[pltpu.VMEM((num_rows + TILE, depth), jnp.float32), pltpu.VMEM((BUFFERS, max(caps), depth), jnp.float32), pltpu.SemaphoreType.DMA, pltpu.SemaphoreType.DMA((BUFFERS,)), pltpu.SemaphoreType.DMA],
+        scratch_shapes=[pltpu.VMEM((num_rows + TILE, depth), jnp.float32), pltpu.VMEM((BUFFERS, max(caps), depth // PARTS), jnp.float32), pltpu.SemaphoreType.DMA((PARTS,)), pltpu.SemaphoreType.DMA((BUFFERS,)), pltpu.SemaphoreType.DMA((PARTS,))],
         compiler_params=pltpu.CompilerParams(vmem_limit_bytes=40 * 2**20),
         cost_estimate=pl.CostEstimate(flops=40 * moved * depth, bytes_accessed=4 * moved * depth, transcendentals=0),
         name='apply_rows',
@@ -256,7 +312,7 @@
         unit = jnp.where(most[2] >= 0, 1.0, 0.0)
         fits = jnp.all(most <= jnp.array(usual, jnp.int32))
 
-        def run(caps, in_shard, out_shard, lent_in, lent_out, owners, ranks, slots, unit):
+        def run(exchange, caps, in_shard, out_shard, lent_in, lent_out, owners, ranks, slots, unit):
             cell_of_id = [owner * cap + rank for owner, rank, cap in zip(owners, ranks, caps)]
             asked = [slot[:, :cap] for slot, cap in zip(slots, caps)]
 
@@ -291,19 +347,24 @@
             ctx_back = send_back(-(pos_grad * center_vec), cell_of_id[1], caps[1])
             in_back = send_back(-(pos_grad * context_vec + d_center_neg), cell_of_id[0], caps[0])
 
-            lent_sum = LEARN_RATE * (jnp.sum(neg_back[:, :TILE], axis=0) + jnp.sum(ctx_back[:, :TILE], axis=0))
-            new_out = apply_rows(out_shard, collect_lent(lent_sum, shards), (asked[2], asked[1]), (neg_back, ctx_back))
-            lent_sum = LEARN_RATE * jnp.sum(in_back[:, :TILE], axis=0)
-            new_in = apply_rows(in_shard, collect_lent(lent_sum, shards), (asked[0],), (in_back,))
+            new_out = apply_rows(out_shard, jnp.zeros((TILE, depth), jnp.float32), (asked[2], asked[1]), (neg_back, ctx_back))
+            sum_out = jnp.sum(neg_back[:, :TILE], axis=0) + jnp.sum(ctx_back[:, :TILE], axis=0)
+            sum_in = jnp.sum(in_back[:, :TILE], axis=0)
+            total = LEARN_RATE * collect_lent(jnp.concatenate([sum_in, sum_out], axis=0), shards)
+            new_in = apply_rows(in_shard, total[:, :TILE].reshape(-1, depth), (asked[0],), (in_back,))
+            new_out = new_out.at[:shards * TILE].add(total[:, TILE:].reshape(-1, depth))
             return new_in, new_out
 
-        def branch(caps):
+        def exchange_full(blocks):
+            return exchange_rows(blocks, 2 + (blocks.shape[1] == full[2]))
+
+        def branch(swap, caps):
             def call(*args):
-                return run(caps, *args)
+                return run(swap, caps, *args)
 
             return call
 
         args = (in_shard, out_shard, lent_in, lent_out, owners, ranks, slots, unit)
-        return lax.cond(fits, branch(usual), branch(full), *args)
+        return lax.cond(fits, branch(exchange, usual), branch(exchange_full, full), *args)
 
     return jax.shard_map(device_step, mesh=mesh, in_specs=(P(AXIS_NAME, None), P(AXIS_NAME, None), P(AXIS_NAME), P(AXIS_NAME), P(AXIS_NAME)), out_specs=(P(AXIS_NAME, None), P(AXIS_NAME, None)), check_vma=False)

time: 1090 us -> 1100 us (level)
  waiting for transfers between devices: 480 us -> 652 us
  Pallas kernels: 270 us -> 104 us
    all_to_all x6, waiting for transfers between devices: 480 us -> 652 us  [exchange(): return lax.all_to_all(blocks, AXIS_NAME, 0, 0)]
    pallas_call x2 -> x1, Pallas kernels: 188 us -> 16.8 us  [collect_lent(): pl.pallas_call(functools.partial(collect_kernel, shards), out_shape=jax.S...]
  transfers between devices with their start and end apart: 6 -> 6, of which waited for: 5 -> 6; matrix products, arithmetic and copies ran while one was open for 23% -> 23% of each run, Pallas kernels for 16% -> 0%
where the time goes in v1:
time: 1100 us; the launch traced here: 1090 us
  waiting for transfers between devices  652 us (59%)
  other arithmetic  123 us (11%)
  local copies, waits for them, and re-layouts  118 us (11%)
  Pallas kernels  104 us (9%)
  matrix products  52.5 us (5%)
  starting transfers between devices  25.9 us (2%)
    all_to_all x6, waiting for transfers between devices, exchange(): return lax.all_to_all(blocks, AXIS_NAME, 0, 0)  652 us
    gather x6, local copies, waits for them, and re-layouts, take_rows(): return rows.at[idx].get(mode='promise_in_bounds')  110 us
    scatter-add x3, other arithmetic, send_back(): jnp.zeros((shards * cap, depth), jnp.float32).at[cells]  91.6 us
    pallas_call x2, Pallas kernels, apply_rows(): pl.pallas_call(functools.partial(apply_kernel, shards, caps, num_rows), o...  66.7 us
    dot_general x15, matrix products, dot_f32(): lax.dot_general(a, b, (dims, ((), ())), preferred_element_type=jnp.float32)  52.5 us
    all_to_all x6, starting transfers between devices, exchange(): return lax.all_to_all(blocks, AXIS_NAME, 0, 0)  25.9 us
  transfers between devices with their start and end apart: 6, of which 6 were waited for; matrix products, arithmetic and copies ran while one was open for 23% of the time, Pallas kernels for 0%

profile of v1, /device:TPU:0, one launch (start us, length us, event | category | flops | bytes accessed | tf_op | source)
XLA Modules:
  0.0 1086.2 jit_solution(10287177851827889454)
XLA Ops:
  7.5 5.5 select_reduce_fusion.1
  18.0 20.2 %ask_owners.1 = (s32[16,8,128]{2,1,0:T(8,128)}, f32[8,2048]{1,0:T(8,128)S(1)}, f32[8,2048]{1,0:T(8,128)S(1)}) custom-call(s32[16,8,128]{2,1,0:T(8,128)} %bitcast.70, f32[2000,2048]{1,0:T(8,128)} %in_shard.1, f32[2000,2048]{1,0:T(8,128)} %out_shard.1), custom_call_target="tpu_custom_call" | custom-call | tf_op jit(solution)/shard_map/ask_owners/pallas_call | solution.py:126
  42.3 1042.8 %conditional.1 = (f32[2000,2048]{1,0:T(8,128)}, f32[2000,2048]{1,0:T(8,128)}) conditional(s32[]{:T(128)} %convert_element_type.174, (s32[16,1024]{1,0:T(8,128)S(1)}, s32[2048]{0:T(1024)S(1)}, s32[2048]{0:T(1024)S(1)}, s32[16,1024]{1,0:T(8,128)S(1)}, f32[2000,2048]{1,0:T(8,128)}, /*index=5*/f32[8,2048]{1,0:T(8,128)S(1)}, s32[16,1024]{1,0:T(8,128)S(1)}, ...), branch_computations={%region_17.25_spmd, %region_25.33_spmd} | conditional | flops 27187564544 | bytes 761600896 | solution.py:368
  48.3 14.5 %gather_fusion.6 = f32[1024,2048]{1,0:T(8,128)} fusion(f32[2000,2048]{1,0:T(8,128)} %get-tuple-element.103.refs_3_, s32[1024]{0:T(1024)S(1)} %broadcast_clamp_fusion.6), kind=kCustom, calls=%fused_computation.6 | custom fusion | bytes 16781312 | tf_op jit(solution)/shard_map/cond/branch_1_fun/gather | solution.py:69
  63.9 4.3 all-to-all-start.2
  68.3 20.0 %gather_fusion.7 = f32[1792,2048]{1,0:T(8,128)} fusion(f32[2000,2048]{1,0:T(8,128)} %get-tuple-element.102.refs_2_, s32[2048]{0:T(1024)S(1)} %pad_clamp_fusion.4), kind=kCustom, calls=%fused_computation.7 | custom fusion | bytes 29367296 | tf_op jit(solution)/shard_map/cond/branch_1_fun/gather | solution.py:69
  89.4 80.4 %all-to-all-done.2 = f32[16,64,2048]{2,1,0:T(8,128)} async-done(((f32[16,64,2048]{2,1,0:T(8,128)}), f32[16,64,2048]{2,1,0:T(8,128)}, u32[]{:S(2)}, u32[]{:S(2)}) %all-to-all-start.2) | async-done | bytes 8388640 | tf_op jit(solution)/shard_map/cond/branch_1_fun/all_to_all | solution.py:65
  169.8 4.3 all-to-all-start
  174.2 20.0 %gather_fusion.9 = f32[1792,2048]{1,0:T(8,128)} fusion(f32[2000,2048]{1,0:T(8,128)} %get-tuple-element.103.refs_3_, s32[2048]{0:T(1024)S(1)} %pad_clamp_fusion.3), kind=kCustom, calls=%fused_computation.9 | custom fusion | bytes 29367296 | tf_op jit(solution)/shard_map/cond/branch_1_fun/gather | solution.py:69
  195.3 154.5 %all-to-all-done = f32[16,112,2048]{2,1,0:T(8,128)} async-done(((f32[16,112,2048]{2,1,0:T(8,128)}), f32[16,112,2048]{2,1,0:T(8,128)}, u32[]{:S(2)}, u32[]{:S(2)}) %all-to-all-start) | async-done | bytes 14680096 | tf_op jit(solution)/shard_map/cond/branch_1_fun/all_to_all | solution.py:65
  349.8 4.4 all-to-all-start.1
  356.0 12.4 %gather_fusion.11 = f32[1024,2048]{1,0:T(8,128)} fusion(f32[1024,2048]{1,0:T(8,128)} %bitcast.17, s32[1024]{0:T(1024)S(1)} %get-tuple-element.158), kind=kCustom, calls=%fused_computation.11 | custom fusion | bytes 16781312 | tf_op jit(solution)/shard_map/cond/branch_1_fun/gather | solution.py:69
  368.4 21.7 %gather_fusion.8 = f32[2048,2048]{1,0:T(8,128)} fusion(f32[1792,2048]{1,0:T(8,128)} %bitcast.14, s32[2048]{0:T(1024)S(1)} %get-tuple-element.160), kind=kCustom, calls=%fused_computation.8 | custom fusion | bytes 33562624 | tf_op jit(solution)/shard_map/cond/branch_1_fun/gather | solution.py:69
  390.1 15.7 %multiply_convert_fusion.4 = bf16[2048,1024]{1,0:T(8,128)(2,1)S(1)} fusion(f32[2048,2048]{1,0:T(8,128)} %gather_fusion.8, f32[1024,2048]{1,0:T(8,128)} %gather_fusion.11, f32[]{:T(128)} %bitcast.18), kind=kOutput, calls=%fused_computation.75 | convolution fusion | flops 8608808960 | bytes 29360132 | tf_op jit(solution)/shard_map/cond/branch_1_fun/dot_general | solution.py:33
  405.8 16.4 %fusion.32 = f32[1024,2048]{1,0:T(8,128)} fusion(bf16[2048,1024]{1,0:T(8,128)(2,1)S(1)} %multiply_convert_fusion.4, f32[2048,2048]{1,0:T(8,128)} %gather_fusion.8), kind=kOutput, calls=%fused_computation.82 | convolution fusion | flops 8594128896 | bytes 29360128 | tf_op jit(solution)/shard_map/cond/branch_1_fun/dot_general | solution.py:33
  422.3 19.5 %scatter_custom_fusion.4 = f32[1024,2048]{1,0:T(8,128)} fusion(s32[1024]{0:T(1024)S(1)} %get-tuple-element.159, f32[1024,2048]{1,0:T(8,128)} %fusion.32, f32[]{:T(128)} %constant.290.clone), kind=kCustom, calls=%fused_computation.73 | custom fusion | flops 4194304 | bytes 16777220 | tf_op jit(solution)/shard_map/cond/branch_1_fun/scatter-add | solution.py:327
  441.8 88.0 %all-to-all-done.1 = f32[16,112,2048]{2,1,0:T(8,128)} async-done(((f32[16,112,2048]{2,1,0:T(8,128)}), f32[16,112,2048]{2,1,0:T(8,128)}, u32[]{:S(2)}, u32[]{:S(2)}) %all-to-all-start.1) | async-done | bytes 14680096 | tf_op jit(solution)/shard_map/cond/branch_1_fun/all_to_all | solution.py:65
  529.8 4.3 all-to-all-start.4
  534.1 21.7 %gather_fusion.10 = f32[2048,2048]{1,0:T(8,128)} fusion(f32[1792,2048]{1,0:T(8,128)} %bitcast.16, s32[2048]{0:T(1024)S(1)} %get-tuple-element.156), kind=kCustom, calls=%fused_computation.10 | custom fusion | bytes 33562624 | tf_op jit(solution)/shard_map/cond/branch_1_fun/gather | solution.py:69
  555.9 11.3 %multiply_reduce_fusion.1 = f32[2048]{0:T(1024)S(1)} fusion(f32[2048,2048]{1,0:T(8,128)} %gather_fusion.8, f32[2048,2048]{1,0:T(8,128)} %gather_fusion.10), kind=kLoop, calls=%fused_computation.72 | loop fusion | flops 8386560 | bytes 33562624 | tf_op jit(solution)/shard_map/cond/branch_1_fun/reduce_sum | solution.py:346
  567.2 35.2 %scatter_custom_fusion.5 = f32[1792,2048]{1,0:T(8,128)} fusion(s32[2048]{0:T(1024)S(1)} %get-tuple-element.157, f32[2048,2048]{1,0:T(8,128)} %gather_fusion.8, f32[2048]{0:T(1024)S(1)} %divide_add_fusion.1, f32[]{:T(128)} %constant.290.clone), kind=kCustom, calls=%fused_computation.65 | custom fusion | flops 12582912 | bytes 31465476 | tf_op jit(solution)/shard_map/cond/branch_1_fun/scatter-add | solution.py:327
  602.4 33.4 %all-to-all-done.4.refs_4_ = f32[16,64,2048]{2,1,0:T(8,128)} async-done(((f32[16,64,2048]{2,1,0:T(8,128)}), f32[16,64,2048]{2,1,0:T(8,128)}, u32[]{:S(2)}, u32[]{:S(2)}) %all-to-all-start.4) | async-done | bytes 8388640 | tf_op jit(solution)/shard_map/cond/branch_1_fun/all_to_all | solution.py:65
  635.8 4.4 all-to-all-start.5
  640.2 15.8 %fusion.35 = f32[2048,2048]{1,0:T(8,128)} fusion(bf16[2048,1024]{1,0:T(8,128)(2,1)} %copy-done.23, f32[1024,2048]{1,0:T(8,128)} %gather_fusion.11, f32[]{:T(128)} %bitcast.18), kind=kOutput, calls=%fused_computation.85 | convolution fusion | flops 8594128896 | bytes 29360132 | tf_op jit(solution)/shard_map/cond/branch_1_fun/dot_general | solution.py:33
  656.0 37.0 %scatter_custom_fusion.3 = f32[1792,2048]{1,0:T(8,128)} fusion(s32[2048]{0:T(1024)} %get-tuple-element.161, f32[2048,2048]{1,0:T(8,128)} %fusion.35, f32[2048,2048]{1,0:T(8,128)} %gather_fusion.10, f32[2048]{0:T(1024)S(1)} %divide_add_fusion.1, f32[]{:T(128)} %constant.290.clone), kind=kCustom, calls=%fused_computation.68 | custom fusion | flops 16777216 | bytes 48243200 | tf_op jit(solution)/shard_map/cond/branch_1_fun/scatter-add | solution.py:327
  692.9 122.9 %all-to-all-done.5.refs_5_ = f32[16,112,2048]{2,1,0:T(8,128)} async-done(((f32[16,112,2048]{2,1,0:T(8,128)}), f32[16,112,2048]{2,1,0:T(8,128)}, u32[]{:S(2)}, u32[]{:S(2)}) %all-to-all-start.5) | async-done | bytes 14680096 | tf_op jit(solution)/shard_map/cond/branch_1_fun/all_to_all | solution.py:65
  815.9 4.1 all-to-all-start.3
  822.8 172.9 %all-to-all-done.3.refs_3_ = f32[16,112,2048]{2,1,0:T(8,128)} async-done(((f32[16,112,2048]{2,1,0:T(8,128)}), f32[16,112,2048]{2,1,0:T(8,128)}, u32[]{:S(2)}, u32[]{:S(2)}) %all-to-all-start.3) | async-done | bytes 14680096 | tf_op jit(solution)/shard_map/cond/branch_1_fun/all_to_all | solution.py:65
  997.7 16.8 %collect_lent.3 = f32[16,16,2048]{2,1,0:T(8,128)} custom-call(f32[16,2048]{1,0:T(8,128)} %pad_maximum_fusion.1.mine), custom_call_target="tpu_custom_call" | custom-call | tf_op jit(solution)/shard_map/cond/branch_1_fun/collect_lent/pallas_call | solution.py:195
  1015.8 39.2 %apply_rows.7 = f32[2000,2048]{1,0:T(8,128)} custom-call(s32[1024]{0:T(1024)S(1)} %reshape.185.refs_0_, s32[1792]{0:T(1024)S(1)} %reshape.186.refs_1_, f32[8,2048]{1,0:T(8,128)S(1)} %broadcast_68_refs_2_.0.refs_2_, f32[2000,2048]{1,0:T(8,128)} %get-tuple-element.103.refs_3_, f32[16,64,2048]{2,1,0:T(8,128)} %all-to-all-done.4.refs_4_, ...), custom_call_target="tpu_custom_call" | custom-call | flops 558366720 | bytes 55836672 | tf_op jit(solution)/shard_map/cond/branch_1_fun/apply_rows/pallas_call | solution.py:281
  1055.0 2.3 fusion.36
  1057.3 27.5 %apply_rows.6 = f32[2000,2048]{1,0:T(8,128)} custom-call(s32[1792]{0:T(1024)S(1)} %reshape.177.refs_0_, f32[128,2048]{1,0:T(8,128)S(1)} %slice_bitcast_fusion.1.refs_1_, f32[2000,2048]{1,0:T(8,128)} %get-tuple-element.102.refs_2_, f32[16,112,2048]{2,1,0:T(8,128)} %all-to-all-done.3.refs_3_), custom_call_target="tpu_custom_call" | custom-call | flops 474480640 | bytes 47448064 | tf_op jit(solution)/shard_map/cond/branch_1_fun/apply_rows/pallas_call | solution.py:281
  (101 shorter events, 25.3 us)
Async XLA Ops:
  18.0 21.1 %copy-start.20 = (s32[3]{0:T(128)S(1)}, s32[3]{0:T(128)}, u32[]{:S(2)}) copy-start(s32[3]{0:T(128)} %constant.319.clone) | copy-start | bytes 40
  46.9 16.0 %copy-start.6 = (s32[2048]{0:T(1024)}, s32[2048]{0:T(1024)S(1)}, u32[]{:S(2)}) copy-start(s32[2048]{0:T(1024)S(1)} %get-tuple-element.113) | copy-start | bytes 24580 | tf_op jit(solution)/shard_map/cond
  46.9 15.9 %copy-start.8 = (s32[2048]{0:T(1024)}, s32[2048]{0:T(1024)S(1)}, u32[]{:S(2)}) copy-start(s32[2048]{0:T(1024)S(1)} %get-tuple-element.112) | copy-start | bytes 24580 | tf_op jit(solution)/shard_map/cond
  63.9 105.9 %all-to-all-start.2 = ((f32[16,64,2048]{2,1,0:T(8,128)}), f32[16,64,2048]{2,1,0:T(8,128)}, u32[]{:S(2)}, u32[]{:S(2)}) async-start(f32[16,64,2048]{2,1,0:T(8,128)} %broadcast_dynamic-update-slice_fusion.5), calls=%async_computation.2 | async-start | bytes 16777216 | tf_op jit(solution)/shard_map/cond/branch_1_fun/all_to_all | solution.py:65
  169.8 180.0 %all-to-all-start = ((f32[16,112,2048]{2,1,0:T(8,128)}), f32[16,112,2048]{2,1,0:T(8,128)}, u32[]{:S(2)}, u32[]{:S(2)}) async-start(f32[16,112,2048]{2,1,0:T(8,128)} %broadcast_dynamic-update-slice_fusion.3), calls=%async_computation | async-start | bytes 29360128 | tf_op jit(solution)/shard_map/cond/branch_1_fun/all_to_all | solution.py:65
  349.8 180.0 %all-to-all-start.1 = ((f32[16,112,2048]{2,1,0:T(8,128)}), f32[16,112,2048]{2,1,0:T(8,128)}, u32[]{:S(2)}, u32[]{:S(2)}) async-start(f32[16,112,2048]{2,1,0:T(8,128)} %broadcast_dynamic-update-slice_fusion.4), calls=%async_computation.1 | async-start | bytes 29360128 | tf_op jit(solution)/shard_map/cond/branch_1_fun/all_to_all | solution.py:65
  405.8 16.5 %copy-start.23 = (bf16[2048,1024]{1,0:T(8,128)(2,1)}, bf16[2048,1024]{1,0:T(8,128)(2,1)S(1)}, u32[]{:S(2)}) copy-start(bf16[2048,1024]{1,0:T(8,128)(2,1)S(1)} %multiply_convert_fusion.4) | copy-start | bytes 12582916 | tf_op jit(solution)/shard_map/cond
  422.3 111.8 %copy-start.7 = (s32[2048]{0:T(1024)S(1)}, s32[2048]{0:T(1024)}, u32[]{:S(2)}) copy-start(s32[2048]{0:T(1024)} %copy-done.6) | copy-start | bytes 24580 | tf_op jit(solution)/shard_map/cond
  422.3 111.8 %copy-start.9 = (s32[2048]{0:T(1024)S(1)}, s32[2048]{0:T(1024)}, u32[]{:S(2)}) copy-start(s32[2048]{0:T(1024)} %copy-done.8) | copy-start | bytes 24580 | tf_op jit(solution)/shard_map/cond
  529.8 106.0 %all-to-all-start.4 = ((f32[16,64,2048]{2,1,0:T(8,128)}), f32[16,64,2048]{2,1,0:T(8,128)}, u32[]{:S(2)}, u32[]{:S(2)}) async-start(f32[16,64,2048]{2,1,0:T(8,128)} %bitcast.62), calls=%async_computation.4 | async-start | bytes 16777216 | tf_op jit(solution)/shard_map/cond/branch_1_fun/all_to_all | solution.py:65
  635.8 180.1 %all-to-all-start.5 = ((f32[16,112,2048]{2,1,0:T(8,128)}), f32[16,112,2048]{2,1,0:T(8,128)}, u32[]{:S(2)}, u32[]{:S(2)}) async-start(f32[16,112,2048]{2,1,0:T(8,128)} %bitcast.58), calls=%async_computation.5 | async-start | bytes 29360128 | tf_op jit(solution)/shard_map/cond/branch_1_fun/all_to_all | solution.py:65
  815.8 4.1 copy-start.16
  815.8 4.2 copy-start.13
  815.8 4.3 copy-start.15
  815.9 179.8 %all-to-all-start.3 = ((f32[16,112,2048]{2,1,0:T(8,128)}), f32[16,112,2048]{2,1,0:T(8,128)}, u32[]{:S(2)}, u32[]{:S(2)}) async-start(f32[16,112,2048]{2,1,0:T(8,128)} %bitcast.60), calls=%async_computation.3 | async-start | bytes 29360128 | tf_op jit(solution)/shard_map/cond/branch_1_fun/all_to_all | solution.py:65
  1015.8 39.2 %copy-start.2 = (f32[16,16,2048]{2,1,0:T(8,128)S(1)}, f32[16,16,2048]{2,1,0:T(8,128)}, u32[]{:S(2)}) copy-start(f32[16,16,2048]{2,1,0:T(8,128)} %collect_lent.3) | copy-start | bytes 6291460 | tf_op jit(solution)/shard_map/cond

commit v2 on v1

--- a/solution.py
+++ b/solution.py
@@ -169,6 +169,97 @@
     )(blocks)
 
 
+def fetch_kernel(shards, in_idx, ctx_idx, neg_blocks, in_shard, out_shard, lent_in, lent_out, neg_got, in_got, in_blocks, ctx_blocks,
+                 held, stage, neg_send, neg_recv, in_send, in_recv, own_sem, load_sem, stage_sem):
+    me = lax.axis_index(AXIS_NAME)
+    load_in = pltpu.make_async_copy(in_shard, held, load_sem)
+    load_in.start()
+    meet(me, shards)
+
+    def exchange(blocks, got, send_sem, recv_sem):
+        count = blocks.shape[1]
+
+        def copy(step, rows):
+            peer = lax.rem(me + step, shards)
+            return remote(blocks.at[peer, rows], got.at[me, rows], send_sem.at[step], recv_sem.at[step], peer)
+
+        def send(tile, carry):
+            for step in range(1, shards):
+                copy(step, pl.ds(pl.multiple_of(tile * TILE, TILE), TILE)).start()
+            return carry
+
+        def finish():
+            for step in range(1, shards):
+                copy(step, pl.ds(0, count)).wait()
+
+        lax.fori_loop(0, count // TILE, send, 0)
+        return finish
+
+    def pick(idx, lent, blocks):
+        count = blocks.shape[1]
+
+        def put(peer, place):
+            return pltpu.make_async_copy(stage.at[place, pl.ds(0, count)], blocks.at[peer], stage_sem.at[place])
+
+        def for_peer(peer, carry):
+            place = lax.rem(peer, 2)
+
+            @pl.when(peer >= 2)
+            def _():
+                put(peer - 2, place).wait()
+
+            stage[place, pl.ds(0, TILE), :] = lent[...]
+
+            def group(step, carry):
+                first = step * TILE
+                for k in range(TILE):
+                    stage[place, pl.ds(first + k, 1), :] = held[pl.ds(idx[peer * count + first + k], 1), :]
+                return carry
+
+            lax.fori_loop(1, count // TILE, group, 0)
+            put(peer, place).start()
+            return carry
+
+        lax.fori_loop(0, shards, for_peer, 0)
+        put(shards - 2, 0).wait()
+        put(shards - 1, 1).wait()
+
+    finish_neg = exchange(neg_blocks, neg_got, neg_send, neg_recv)
+    own_neg = pltpu.make_async_copy(neg_blocks.at[me], neg_got.at[me], own_sem.at[0])
+    own_neg.start()
+    load_in.wait()
+    pick(in_idx, lent_in, in_blocks)
+    finish_in = exchange(in_blocks, in_got, in_send, in_recv)
+    own_in = pltpu.make_async_copy(in_blocks.at[me], in_got.at[me], own_sem.at[1])
+    own_in.start()
+    load_out = pltpu.make_async_copy(out_shard, held, load_sem)
+    load_out.start()
+    load_out.wait()
+    pick(ctx_idx, lent_out, ctx_blocks)
+    own_neg.wait()
+    own_in.wait()
+    finish_neg()
+    finish_in()
+
+
+def fetch_rows(in_slot, ctx_slot, neg_blocks, in_shard, out_shard, lent_in, lent_out, collective_id):
+    shards, in_cap = in_slot.shape
+    ctx_cap, depth = ctx_slot.shape[1], in_shard.shape[1]
+    smem, vmem, any_space = (pl.BlockSpec(memory_space=space) for space in (pltpu.SMEM, pltpu.VMEM, pl.ANY))
+    in_shape = jax.ShapeDtypeStruct((shards, in_cap, depth), jnp.float32)
+    ctx_shape = jax.ShapeDtypeStruct((shards, ctx_cap, depth), jnp.float32)
+    sems = pltpu.SemaphoreType.DMA((shards,))
+    neg_got, in_got, _, ctx_blocks = pl.pallas_call(
+        functools.partial(fetch_kernel, shards),
+        out_shape=(jax.ShapeDtypeStruct(neg_blocks.shape, jnp.float32), in_shape, in_shape, ctx_shape),
+        in_specs=[smem, smem, any_space, any_space, any_space, vmem, vmem],
+        out_specs=(any_space,) * 4,
+        scratch_shapes=[pltpu.VMEM(in_shard.shape, jnp.float32), pltpu.VMEM((2, max(in_cap, ctx_cap), depth), jnp.float32), sems, sems, sems, sems, pltpu.SemaphoreType.DMA((2,)), pltpu.SemaphoreType.DMA, pltpu.SemaphoreType.DMA((2,))],
+        compiler_params=pltpu.CompilerParams(collective_id=collective_id, has_side_effects=True, vmem_limit_bytes=40 * 2**20),
+    )(jnp.maximum(in_slot - TILE, 0).reshape(-1), jnp.maximum(ctx_slot - TILE, 0).reshape(-1), neg_blocks, in_shard, out_shard, lent_in, lent_out)
+    return neg_got.reshape(-1, depth), in_got.reshape(-1, depth), ctx_blocks
+
+
 def collect_kernel(shards, mine, got, send_sem, recv_sem):
     me = lax.axis_index(AXIS_NAME)
     ready = pltpu.get_barrier_semaphore()
@@ -309,10 +400,9 @@
         edge1, edge2, edge3 = full[0], full[0] + full[1], sum(full)
         slots = (arrived[:, :edge1], arrived[:, edge1:edge2], arrived[:, edge2:edge3])
         most = jnp.max(arrived[:, edge3:edge3 + 3], axis=0)
-        unit = jnp.where(most[2] >= 0, 1.0, 0.0)
         fits = jnp.all(most <= jnp.array(usual, jnp.int32))
 
-        def run(exchange, caps, in_shard, out_shard, lent_in, lent_out, owners, ranks, slots, unit):
+        def run(exchange, caps, in_shard, out_shard, lent_in, lent_out, owners, ranks, slots):
             cell_of_id = [owner * cap + rank for owner, rank, cap in zip(owners, ranks, caps)]
             asked = [slot[:, :cap] for slot, cap in zip(slots, caps)]
 
@@ -320,20 +410,15 @@
                 rows = take_rows(table, jnp.maximum(slot - TILE, 0))
                 return lax.dynamic_update_slice(rows, jnp.broadcast_to(lent[None], (shards, TILE, depth)), (0, 0, 0))
 
-            def fetch(rows):
-                return exchange(rows).reshape(-1, depth)
-
             def send_back(grads, cells, cap):
                 summed = jnp.zeros((shards * cap, depth), jnp.float32).at[cells].add(grads, mode='promise_in_bounds')
                 return exchange(summed.reshape(shards, cap, depth))
 
-            picked_neg, slot_in, slot_ctx = lax.optimization_barrier((pick(out_shard, lent_out, asked[2]), asked[0], asked[1]))
-            neg_rows = fetch(picked_neg)
-            picked_in, slot_ctx = lax.optimization_barrier((pick(in_shard, lent_in, slot_in), slot_ctx))
-            in_rows = fetch(picked_in)
-            ctx_rows = fetch(pick(out_shard, lent_out, slot_ctx))
-
-            negative_half = (take_rows(neg_rows, cell_of_id[2]) * unit).astype(jnp.bfloat16)
+            picked = pick(out_shard, lent_out, asked[2])
+            neg_rows, in_rows, ctx_blocks = fetch_rows(asked[0], asked[1], picked, in_shard, out_shard, lent_in, lent_out, 4 if caps == usual else 5)
+            ctx_rows = exchange(ctx_blocks).reshape(-1, depth)
+
+            negative_half = take_rows(neg_rows, cell_of_id[2]).astype(jnp.bfloat16)
             center_vec = take_rows(in_rows, cell_of_id[0])
             center_half = center_vec.astype(jnp.bfloat16)
             neg_score = dot_f32(center_half, negative_half, ((1,), (1,)))
@@ -364,7 +449,7 @@
 
             return call
 
-        args = (in_shard, out_shard, lent_in, lent_out, owners, ranks, slots, unit)
+        args = (in_shard, out_shard, lent_in, lent_out, owners, ranks, slots)
         return lax.cond(fits, branch(exchange, usual), branch(exchange_full, full), *args)
 
     return jax.shard_map(device_step, mesh=mesh, in_specs=(P(AXIS_NAME, None), P(AXIS_NAME, None), P(AXIS_NAME), P(AXIS_NAME), P(AXIS_NAME)), out_specs=(P(AXIS_NAME, None), P(AXIS_NAME, None)), check_vma=False)

time: 1100 us -> 1080 us (0.982)
  Pallas kernels: 104 us -> 363 us
  waiting for transfers between devices: 652 us -> 421 us
  local copies, waits for them, and re-layouts: 118 us -> 78.9 us
    pallas_call x0 -> x1, Pallas kernels: none -> 260 us  [fetch_rows(): pl.pallas_call(functools.partial(fetch_kernel, shards), out_shape=(jax.Sh...]
    all_to_all x6 -> x4, waiting for transfers between devices: 652 us -> 421 us  [exchange(): return lax.all_to_all(blocks, AXIS_NAME, 0, 0)]
    gather x6 -> x4, local copies, waits for them, and re-layouts: 110 us -> 70.2 us  [take_rows(): return rows.at[idx].get(mode='promise_in_bounds')]
    all_to_all x6 -> x4, starting transfers between devices: 25.9 us -> 17.1 us  [exchange(): return lax.all_to_all(blocks, AXIS_NAME, 0, 0)]
  transfers between devices with their start and end apart: 6 -> 4, of which waited for: 6 -> 4; matrix products, arithmetic and copies ran while one was open for 23% -> 19% of each run, Pallas kernels for 0% -> 0%
where the time goes in v2:
time: 1080 us; the launch traced here: 1070 us
  waiting for transfers between devices  421 us (39%)
  Pallas kernels  363 us (34%)
  other arithmetic  123 us (11%)
  local copies, waits for them, and re-layouts  78.9 us (7%)
  matrix products  50.2 us (5%)
  starting transfers between devices  17.1 us (2%)
    all_to_all x4, waiting for transfers between devices, exchange(): return lax.all_to_all(blocks, AXIS_NAME, 0, 0)  421 us
    pallas_call x1, Pallas kernels, fetch_rows(): pl.pallas_call(functools.partial(fetch_kernel, shards), out_shape=(jax.Sh...  260 us
    scatter-add x3, other arithmetic, send_back(): jnp.zeros((shards * cap, depth), jnp.float32).at[cells]  91.4 us
    gather x4, local copies, waits for them, and re-layouts, take_rows(): return rows.at[idx].get(mode='promise_in_bounds')  70.2 us
    pallas_call x2, Pallas kernels, apply_rows(): pl.pallas_call(functools.partial(apply_kernel, shards, caps, num_rows), o...  66.7 us
    dot_general x15, matrix products, dot_f32(): lax.dot_general(a, b, (dims, ((), ())), preferred_element_type=jnp.float32)  50.2 us
  transfers between devices with their start and end apart: 4, of which 4 were waited for; matrix products, arithmetic and copies ran while one was open for 19% of the time, Pallas kernels for 0%

profile of v2, /device:TPU:0, one launch (start us, length us, event | category | flops | bytes accessed | tf_op | source)
XLA Modules:
  0.0 1068.0 jit_solution(12953655768832435601)
XLA Ops:
  2.5 1.6 select_reduce_fusion.2
  7.5 5.5 select_reduce_fusion.1
  18.0 20.2 %ask_owners.1 = (s32[16,8,128]{2,1,0:T(8,128)}, f32[8,2048]{1,0:T(8,128)S(1)}, f32[8,2048]{1,0:T(8,128)S(1)}) custom-call(s32[16,8,128]{2,1,0:T(8,128)} %bitcast.66, f32[2000,2048]{1,0:T(8,128)} %in_shard.1, f32[2000,2048]{1,0:T(8,128)} %out_shard.1), custom_call_target="tpu_custom_call" | custom-call | tf_op jit(solution)/shard_map/ask_owners/pallas_call | solution.py:126
  42.3 1024.4 %conditional.1 = (f32[2000,2048]{1,0:T(8,128)}, f32[2000,2048]{1,0:T(8,128)}) conditional(s32[]{:T(128)} %convert_element_type.174, (s32[16,1024]{1,0:T(8,128)S(1)}, s32[2048]{0:T(1024)S(1)}, s32[2048]{0:T(1024)S(1)}, s32[16,1024]{1,0:T(8,128)S(1)}, s32[16,1024]{1,0:T(8,128)S(1)}, /*index=5*/f32[2000,2048]{1,0:T(8,128)}, f32[8,2048]{1,0:T(8,128)S(1)}, ...), branch_computations={%region_17.25_spmd, %region_25.33_spmd} | conditional | flops 27179161600 | bytes 649291904 | solution.py:453
  53.1 14.5 %gather_fusion.4 = f32[1024,2048]{1,0:T(8,128)} fusion(f32[2000,2048]{1,0:T(8,128)} %get-tuple-element.96.out_shard.refs_3_, s32[1024]{0:T(1024)S(1)} %broadcast_clamp_fusion.6), kind=kCustom, calls=%fused_computation.4 | custom fusion | bytes 16781312 | tf_op jit(solution)/shard_map/cond/branch_1_fun/gather | solution.py:69
  68.6 259.7 %branch_1_fun.1 = (f32[16,64,2048]{2,1,0:T(8,128)S(1)}, f32[16,112,2048]{2,1,0:T(8,128)}, f32[16,112,2048]{2,1,0:T(8,128)}, f32[16,112,2048]{2,1,0:T(8,128)}) custom-call(s32[1792]{0:T(1024)S(1)} %reshape.181.in_idx, s32[1792]{0:T(1024)S(1)} %reshape.182.ctx_idx, f32[16,64,2048]{2,1,0:T(8,128)} %broadcast_dynamic-update-slice_fusion.1.neg_blocks, ...), custom_call_target="tpu_custom_call" | custom-call | tf_op jit(solution)/shard_map/cond/branch_1_fun/pallas_call | solution.py:252
  328.3 3.4 copy-done
  331.7 3.8 all-to-all-start
  336.2 21.7 %gather_fusion.5 = f32[2048,2048]{1,0:T(8,128)} fusion(f32[1792,2048]{1,0:T(8,128)} %bitcast.47, s32[2048]{0:T(1024)S(1)} %get-tuple-element.162), kind=kCustom, calls=%fused_computation.5 | custom fusion | bytes 33562624 | tf_op jit(solution)/shard_map/cond/branch_1_fun/gather | solution.py:69
  357.9 12.2 %gather_fusion.7 = bf16[1024,2048]{1,0:T(8,128)(2,1)} fusion(f32[1024,2048]{1,0:T(8,128)} %bitcast.46, s32[1024]{0:T(1024)S(1)} %get-tuple-element.134), kind=kCustom, calls=%fused_computation.7 | custom fusion | bytes 8392704 | tf_op jit(solution)/shard_map/cond/branch_1_fun/gather | solution.py:69
  370.2 14.5 %multiply_convert_fusion.1 = bf16[2048,1024]{1,0:T(8,128)(2,1)S(1)} fusion(f32[2048,2048]{1,0:T(8,128)} %gather_fusion.5, bf16[1024,2048]{1,0:T(8,128)(2,1)} %gather_fusion.7), kind=kOutput, calls=%fused_computation.70 | convolution fusion | flops 8604614656 | bytes 25165824 | tf_op jit(solution)/shard_map/cond/branch_1_fun/dot_general | solution.py:33
  384.6 16.1 %fusion.36 = f32[1024,2048]{1,0:T(8,128)} fusion(bf16[2048,1024]{1,0:T(8,128)(2,1)S(1)} %multiply_convert_fusion.1, f32[2048,2048]{1,0:T(8,128)} %gather_fusion.5), kind=kOutput, calls=%fused_computation.76 | convolution fusion | flops 8594128896 | bytes 29360128 | tf_op jit(solution)/shard_map/cond/branch_1_fun/dot_general | solution.py:33
  400.7 19.3 %scatter_custom_fusion.4 = f32[1024,2048]{1,0:T(8,128)} fusion(s32[1024]{0:T(1024)S(1)} %get-tuple-element.135, f32[1024,2048]{1,0:T(8,128)} %fusion.36, f32[]{:T(128)} %constant.276.clone), kind=kCustom, calls=%fused_computation.68 | custom fusion | flops 4194304 | bytes 16777220 | tf_op jit(solution)/shard_map/cond/branch_1_fun/scatter-add | solution.py:414
  420.0 90.9 %all-to-all-done = f32[16,112,2048]{2,1,0:T(8,128)} async-done(((f32[16,112,2048]{2,1,0:T(8,128)}), f32[16,112,2048]{2,1,0:T(8,128)}, u32[]{:S(2)}, u32[]{:S(2)}) %all-to-all-start) | async-done | bytes 14680096 | tf_op jit(solution)/shard_map/cond/branch_1_fun/all_to_all | solution.py:65
  510.9 4.6 all-to-all-start.2
  515.6 21.7 %gather_fusion.6 = f32[2048,2048]{1,0:T(8,128)} fusion(f32[1792,2048]{1,0:T(8,128)} %bitcast.11, s32[2048]{0:T(1024)S(1)} %get-tuple-element.132), kind=kCustom, calls=%fused_computation.6 | custom fusion | bytes 33562624 | tf_op jit(solution)/shard_map/cond/branch_1_fun/gather | solution.py:69
  537.3 11.3 %multiply_reduce_fusion.1 = f32[2048]{0:T(1024)S(1)} fusion(f32[2048,2048]{1,0:T(8,128)} %gather_fusion.5, f32[2048,2048]{1,0:T(8,128)} %gather_fusion.6), kind=kLoop, calls=%fused_computation.67 | loop fusion | flops 8386560 | bytes 33562624 | tf_op jit(solution)/shard_map/cond/branch_1_fun/reduce_sum | solution.py:431
  548.6 35.2 %scatter_custom_fusion.5 = f32[1792,2048]{1,0:T(8,128)} fusion(s32[2048]{0:T(1024)} %get-tuple-element.133, f32[2048,2048]{1,0:T(8,128)} %gather_fusion.5, f32[2048]{0:T(1024)S(1)} %divide_add_fusion.1, f32[]{:T(128)} %constant.276.clone), kind=kCustom, calls=%fused_computation.60 | custom fusion | flops 12582912 | bytes 31465984 | tf_op jit(solution)/shard_map/cond/branch_1_fun/scatter-add | solution.py:414
  583.8 33.5 %all-to-all-done.2.refs_4_ = f32[16,64,2048]{2,1,0:T(8,128)} async-done(((f32[16,64,2048]{2,1,0:T(8,128)}), f32[16,64,2048]{2,1,0:T(8,128)}, u32[]{:S(2)}, u32[]{:S(2)}) %all-to-all-start.2) | async-done | bytes 8388640 | tf_op jit(solution)/shard_map/cond/branch_1_fun/all_to_all | solution.py:65
  617.2 4.5 all-to-all-start.3
  621.7 15.1 %fusion.107 = f32[2048,2048]{1,0:T(8,128)} fusion(bf16[2048,1024]{1,0:T(8,128)(2,1)} %copy-done.11, bf16[1024,2048]{1,0:T(8,128)(2,1)} %gather_fusion.7), kind=kOutput, calls=%fused_computation.253 | convolution fusion | flops 8589934592 | bytes 25165824 | tf_op jit(solution)/shard_map/cond/branch_1_fun/dot_general | solution.py:33
  636.8 37.0 %scatter_custom_fusion.3 = f32[1792,2048]{1,0:T(8,128)} fusion(s32[2048]{0:T(1024)} %get-tuple-element.163, f32[2048,2048]{1,0:T(8,128)} %fusion.107, f32[2048,2048]{1,0:T(8,128)} %gather_fusion.6, f32[2048]{0:T(1024)S(1)} %divide_add_fusion.1, f32[]{:T(128)} %constant.276.clone), kind=kCustom, calls=%fused_computation.63 | custom fusion | flops 16777216 | bytes 48243200 | tf_op jit(solution)/shard_map/cond/branch_1_fun/scatter-add | solution.py:414
  673.8 123.5 %all-to-all-done.3.refs_5_ = f32[16,112,2048]{2,1,0:T(8,128)} async-done(((f32[16,112,2048]{2,1,0:T(8,128)}), f32[16,112,2048]{2,1,0:T(8,128)}, u32[]{:S(2)}, u32[]{:S(2)}) %all-to-all-start.3) | async-done | bytes 14680096 | tf_op jit(solution)/shard_map/cond/branch_1_fun/all_to_all | solution.py:65
  797.3 4.1 all-to-all-start.1
  801.7 1.3 slice_reduce_fusion.4
  803.0 1.3 slice_reduce_fusion.3
  804.3 172.9 %all-to-all-done.1.refs_3_ = f32[16,112,2048]{2,1,0:T(8,128)} async-done(((f32[16,112,2048]{2,1,0:T(8,128)}), f32[16,112,2048]{2,1,0:T(8,128)}, u32[]{:S(2)}, u32[]{:S(2)}) %all-to-all-start.1) | async-done | bytes 14680096 | tf_op jit(solution)/shard_map/cond/branch_1_fun/all_to_all | solution.py:65
  979.2 16.8 %collect_lent.3 = f32[16,16,2048]{2,1,0:T(8,128)} custom-call(f32[16,2048]{1,0:T(8,128)} %pad_maximum_fusion.1.mine), custom_call_target="tpu_custom_call" | custom-call | tf_op jit(solution)/shard_map/cond/branch_1_fun/collect_lent/pallas_call | solution.py:286
  995.9 1.3 slice_bitcast_fusion.1.refs_1_
  997.3 39.2 %apply_rows.7 = f32[2000,2048]{1,0:T(8,128)} custom-call(s32[1024]{0:T(1024)S(1)} %reshape.190.refs_0_, s32[1792]{0:T(1024)S(1)} %reshape.191.refs_1_, f32[8,2048]{1,0:T(8,128)S(1)} %broadcast_65_refs_2_.0.refs_2_, f32[2000,2048]{1,0:T(8,128)} %get-tuple-element.96.out_shard.refs_3_, f32[16,64,2048]{2,1,0:T(8,128)} %all-to-all-done.2.refs_4_, ...), custom_call_target="tpu_custom_call" | custom-call | flops 558366720 | bytes 55836672 | tf_op jit(solution)/shard_map/cond/branch_1_fun/apply_rows/pallas_call | solution.py:372
  1036.5 2.3 fusion.42
  1038.8 27.5 %apply_rows.6 = f32[2000,2048]{1,0:T(8,128)} custom-call(s32[1792]{0:T(1024)S(1)} %reshape.180.refs_0_, f32[128,2048]{1,0:T(8,128)S(1)} %slice_bitcast_fusion.1.refs_1_, f32[2000,2048]{1,0:T(8,128)} %get-tuple-element.99.in_shard.refs_2_, f32[16,112,2048]{2,1,0:T(8,128)} %all-to-all-done.1.refs_3_), custom_call_target="tpu_custom_call" | custom-call | flops 474480640 | bytes 47448064 | tf_op jit(solution)/shard_map/cond/branch_1_fun/apply_rows/pallas_call | solution.py:372
  (82 shorter events, 17.1 us)
Async XLA Ops:
  18.0 21.1 %copy-start.10 = (s32[3]{0:T(128)S(1)}, s32[3]{0:T(128)}, u32[]{:S(2)}) copy-start(s32[3]{0:T(128)} %constant.302.clone) | copy-start | bytes 40
  328.3 3.4 copy-start
  331.7 179.2 %all-to-all-start = ((f32[16,112,2048]{2,1,0:T(8,128)}), f32[16,112,2048]{2,1,0:T(8,128)}, u32[]{:S(2)}, u32[]{:S(2)}) async-start(f32[16,112,2048]{2,1,0:T(8,128)} %get-tuple-element.102), calls=%async_computation | async-start | bytes 29360128 | tf_op jit(solution)/shard_map/cond/branch_1_fun/all_to_all | solution.py:65
  384.6 16.1 %copy-start.11 = (bf16[2048,1024]{1,0:T(8,128)(2,1)}, bf16[2048,1024]{1,0:T(8,128)(2,1)S(1)}, u32[]{:S(2)}) copy-start(bf16[2048,1024]{1,0:T(8,128)(2,1)S(1)} %multiply_convert_fusion.1) | copy-start | bytes 12582916 | tf_op jit(solution)/shard_map/cond
  510.9 106.3 %all-to-all-start.2 = ((f32[16,64,2048]{2,1,0:T(8,128)}), f32[16,64,2048]{2,1,0:T(8,128)}, u32[]{:S(2)}, u32[]{:S(2)}) async-start(f32[16,64,2048]{2,1,0:T(8,128)} %bitcast.57), calls=%async_computation.2 | async-start | bytes 16777216 | tf_op jit(solution)/shard_map/cond/branch_1_fun/all_to_all | solution.py:65
  617.2 180.1 %all-to-all-start.3 = ((f32[16,112,2048]{2,1,0:T(8,128)}), f32[16,112,2048]{2,1,0:T(8,128)}, u32[]{:S(2)}, u32[]{:S(2)}) async-start(f32[16,112,2048]{2,1,0:T(8,128)} %bitcast.54), calls=%async_computation.3 | async-start | bytes 29360128 | tf_op jit(solution)/shard_map/cond/branch_1_fun/all_to_all | solution.py:65
  797.3 4.1 copy-start.9
  797.3 4.2 copy-start.6
  797.3 4.3 copy-start.8
  797.3 179.8 %all-to-all-start.1 = ((f32[16,112,2048]{2,1,0:T(8,128)}), f32[16,112,2048]{2,1,0:T(8,128)}, u32[]{:S(2)}, u32[]{:S(2)}) async-start(f32[16,112,2048]{2,1,0:T(8,128)} %bitcast.56), calls=%async_computation.1 | async-start | bytes 29360128 | tf_op jit(solution)/shard_map/cond/branch_1_fun/all_to_all | solution.py:65
  997.3 39.2 %copy-start.3 = (f32[16,16,2048]{2,1,0:T(8,128)S(1)}, f32[16,16,2048]{2,1,0:T(8,128)}, u32[]{:S(2)}) copy-start(f32[16,16,2048]{2,1,0:T(8,128)} %collect_lent.3) | copy-start | bytes 6291460 | tf_op jit(solution)/shard_map/cond

commit v3 on v2

--- a/solution.py
+++ b/solution.py
@@ -169,7 +169,7 @@
     )(blocks)
 
 
-def fetch_kernel(shards, in_idx, ctx_idx, neg_blocks, in_shard, out_shard, lent_in, lent_out, neg_got, in_got, in_blocks, ctx_blocks,
+def fetch_kernel(shards, in_idx, ctx_idx, neg_blocks, in_shard, out_shard, lent_in, neg_got, in_got, in_blocks, ctx_blocks,
                  held, stage, neg_send, neg_recv, in_send, in_recv, own_sem, load_sem, stage_sem):
     me = lax.axis_index(AXIS_NAME)
     load_in = pltpu.make_async_copy(in_shard, held, load_sem)
@@ -208,7 +208,8 @@
             def _():
                 put(peer - 2, place).wait()
 
-            stage[place, pl.ds(0, TILE), :] = lent[...]
+            if lent is not None:
+                stage[place, pl.ds(0, TILE), :] = lent[...]
 
             def group(step, carry):
                 first = step * TILE
@@ -216,7 +217,7 @@
                     stage[place, pl.ds(first + k, 1), :] = held[pl.ds(idx[peer * count + first + k], 1), :]
                 return carry
 
-            lax.fori_loop(1, count // TILE, group, 0)
+            lax.fori_loop(0 if lent is None else 1, count // TILE, group, 0)
             put(peer, place).start()
             return carry
 
@@ -235,14 +236,14 @@
     load_out = pltpu.make_async_copy(out_shard, held, load_sem)
     load_out.start()
     load_out.wait()
-    pick(ctx_idx, lent_out, ctx_blocks)
+    pick(ctx_idx, None, ctx_blocks)
     own_neg.wait()
     own_in.wait()
     finish_neg()
     finish_in()
 
 
-def fetch_rows(in_slot, ctx_slot, neg_blocks, in_shard, out_shard, lent_in, lent_out, collective_id):
+def fetch_rows(in_slot, ctx_slot, neg_blocks, in_shard, out_shard, lent_in, collective_id):
     shards, in_cap = in_slot.shape
     ctx_cap, depth = ctx_slot.shape[1], in_shard.shape[1]
     smem, vmem, any_space = (pl.BlockSpec(memory_space=space) for space in (pltpu.SMEM, pltpu.VMEM, pl.ANY))
@@ -252,11 +253,11 @@
     neg_got, in_got, _, ctx_blocks = pl.pallas_call(
         functools.partial(fetch_kernel, shards),
         out_shape=(jax.ShapeDtypeStruct(neg_blocks.shape, jnp.float32), in_shape, in_shape, ctx_shape),
-        in_specs=[smem, smem, any_space, any_space, any_space, vmem, vmem],
+        in_specs=[smem, smem, any_space, any_space, any_space, vmem],
         out_specs=(any_space,) * 4,
         scratch_shapes=[pltpu.VMEM(in_shard.shape, jnp.float32), pltpu.VMEM((2, max(in_cap, ctx_cap), depth), jnp.float32), sems, sems, sems, sems, pltpu.SemaphoreType.DMA((2,)), pltpu.SemaphoreType.DMA, pltpu.SemaphoreType.DMA((2,))],
         compiler_params=pltpu.CompilerParams(collective_id=collective_id, has_side_effects=True, vmem_limit_bytes=40 * 2**20),
-    )(jnp.maximum(in_slot - TILE, 0).reshape(-1), jnp.maximum(ctx_slot - TILE, 0).reshape(-1), neg_blocks, in_shard, out_shard, lent_in, lent_out)
+    )(jnp.maximum(in_slot - TILE, 0).reshape(-1), jnp.maximum(ctx_slot - TILE, 0).reshape(-1), neg_blocks, in_shard, out_shard, lent_in)
     return neg_got.reshape(-1, depth), in_got.reshape(-1, depth), ctx_blocks
 
 
@@ -299,7 +300,7 @@
 PARTS = 2
 
 
-def apply_kernel(shards, caps, num_rows, *refs):
+def apply_kernel(shards, caps, skips, num_rows, *refs):
     lists = len(caps)
     rows, (lent, table), grads, out = refs[:lists], refs[lists:lists + 2], refs[lists + 2:2 * lists + 2], refs[2 * lists + 2]
     total, buf, load_sem, grad_sem, store_sem = refs[2 * lists + 3:]
@@ -353,7 +354,7 @@
                     total[pl.ds(idx[k], 1), columns(part)] = sums[k]
                 return carry
 
-            return lax.fori_loop(TILE // GROUP, caps[i] // GROUP, group, carry)
+            return lax.fori_loop(skips[i] // GROUP, caps[i] // GROUP, group, carry)
 
         lax.fori_loop(0, shards, from_source, 0)
         if i == lists - 1:
@@ -362,7 +363,7 @@
         store(part).wait()
 
 
-def apply_rows(table, lent, slots, grads):
+def apply_rows(table, lent, slots, grads, skips):
     num_rows, depth = table.shape
     shards = grads[0].shape[0]
     caps = tuple(g.shape[1] for g in grads)
@@ -370,7 +371,7 @@
     any_space = pl.BlockSpec(memory_space=pl.ANY)
     moved = 2 * num_rows + sum(caps) * shards
     return pl.pallas_call(
-        functools.partial(apply_kernel, shards, caps, num_rows),
+        functools.partial(apply_kernel, shards, caps, skips, num_rows),
         out_shape=jax.ShapeDtypeStruct(table.shape, jnp.float32),
         in_specs=[pl.BlockSpec(memory_space=pltpu.SMEM)] * len(caps) + [pl.BlockSpec(memory_space=pltpu.VMEM), any_space] + [any_space] * len(caps),
         out_specs=any_space,
@@ -402,46 +403,63 @@
         most = jnp.max(arrived[:, edge3:edge3 + 3], axis=0)
         fits = jnp.all(most <= jnp.array(usual, jnp.int32))
 
-        def run(exchange, caps, in_shard, out_shard, lent_in, lent_out, owners, ranks, slots):
-            cell_of_id = [owner * cap + rank for owner, rank, cap in zip(owners, ranks, caps)]
+        def onehot_f32(ids):
+            return (ids[:, None] == lax.broadcasted_iota(jnp.int32, (1, shards * TILE), 1)).astype(jnp.float32)
+
+        def lent_product(a, b, dims):
+            return lax.dot_general(a, b, (dims, ((), ())), precision=lax.Precision.HIGHEST)
+
+        def run(exchange, caps, in_shard, out_shard, lent_in, lent_out, context_ids, negative_ids, owners, ranks, slots):
             asked = [slot[:, :cap] for slot, cap in zip(slots, caps)]
 
             def pick(table, lent, slot):
                 rows = take_rows(table, jnp.maximum(slot - TILE, 0))
                 return lax.dynamic_update_slice(rows, jnp.broadcast_to(lent[None], (shards, TILE, depth)), (0, 0, 0))
 
-            def send_back(grads, cells, cap):
-                summed = jnp.zeros((shards * cap, depth), jnp.float32).at[cells].add(grads, mode='promise_in_bounds')
-                return exchange(summed.reshape(shards, cap, depth))
+            def send_back(start, cells, grads):
+                summed = start.reshape(-1, depth).at[cells].add(grads, mode='drop')
+                return exchange(summed.reshape(start.shape))
+
+            in_cap, ctx_cap, neg_cap = caps
+            in_cell = owners[0] * in_cap + ranks[0]
+            ctx_cell = owners[1] * ctx_cap + ranks[1]
+            ctx_cold = jnp.maximum(ctx_cell - TILE * (owners[1] + 1), 0)
+            neg_cell = owners[2] * neg_cap + ranks[2]
+            neg_cold = jnp.where(ranks[2] < TILE, shards * (neg_cap - TILE), neg_cell - TILE * (owners[2] + 1))
 
             picked = pick(out_shard, lent_out, asked[2])
-            neg_rows, in_rows, ctx_blocks = fetch_rows(asked[0], asked[1], picked, in_shard, out_shard, lent_in, lent_out, 4 if caps == usual else 5)
+            neg_rows, in_rows, ctx_blocks = fetch_rows(asked[0], asked[1][:, TILE:], picked, in_shard, out_shard, lent_in, 4 if caps == usual else 5)
             ctx_rows = exchange(ctx_blocks).reshape(-1, depth)
 
-            negative_half = take_rows(neg_rows, cell_of_id[2]).astype(jnp.bfloat16)
-            center_vec = take_rows(in_rows, cell_of_id[0])
+            negative_half = take_rows(neg_rows, neg_cell).astype(jnp.bfloat16)
+            center_vec = take_rows(in_rows, in_cell)
             center_half = center_vec.astype(jnp.bfloat16)
             neg_score = dot_f32(center_half, negative_half, ((1,), (1,)))
             neg_grad = ((NEG_WEIGHT / num_negs) * jax.nn.sigmoid(neg_score)).astype(jnp.bfloat16)
             d_negative = -dot_f32(neg_grad, center_half, ((0,), (0,)))
-            neg_back = send_back(d_negative, cell_of_id[2], caps[2])
+            neg_back = send_back(jnp.zeros((shards, neg_cap - TILE, depth), jnp.float32), neg_cold, d_negative)
             d_center_neg = dot_f32(neg_grad, negative_half, ((1,), (0,)))
-
-            context_vec = take_rows(ctx_rows, cell_of_id[1])
+            lent_neg = lent_product(onehot_f32(negative_ids), d_negative, ((0,), (0,)))
+            lent_rows = neg_rows.reshape(shards, neg_cap, depth)[:, :TILE].reshape(-1, depth)
+            lent_ctx = lent_product(onehot_f32(context_ids), lent_rows, ((1,), (0,)))
+            lent_ctx, d_center_neg = lax.optimization_barrier((lent_ctx, d_center_neg))
+
+            context_vec = jnp.where((ranks[1] < TILE)[:, None], lent_ctx, take_rows(ctx_rows, ctx_cold))
             pos_grad = (jax.nn.sigmoid(jnp.sum(center_vec * context_vec, axis=1)) - 1.0)[:, None]
-            ctx_back = send_back(-(pos_grad * center_vec), cell_of_id[1], caps[1])
-            in_back = send_back(-(pos_grad * context_vec + d_center_neg), cell_of_id[0], caps[0])
-
-            new_out = apply_rows(out_shard, jnp.zeros((TILE, depth), jnp.float32), (asked[2], asked[1]), (neg_back, ctx_back))
-            sum_out = jnp.sum(neg_back[:, :TILE], axis=0) + jnp.sum(ctx_back[:, :TILE], axis=0)
-            sum_in = jnp.sum(in_back[:, :TILE], axis=0)
-            total = LEARN_RATE * collect_lent(jnp.concatenate([sum_in, sum_out], axis=0), shards)
-            new_in = apply_rows(in_shard, total[:, :TILE].reshape(-1, depth), (asked[0],), (in_back,))
+            start = jnp.pad(lent_neg.reshape(shards, TILE, depth), ((0, 0), (0, ctx_cap - TILE), (0, 0)))
+            ctx_back = send_back(start, ctx_cell, -(pos_grad * center_vec))
+            in_back = send_back(jnp.zeros((shards, in_cap, depth), jnp.float32), in_cell, -(pos_grad * context_vec + d_center_neg))
+
+            new_out = apply_rows(out_shard, jnp.zeros((TILE, depth), jnp.float32), (asked[2][:, TILE:], asked[1]), (neg_back, ctx_back), (0, TILE))
+            sums = [jnp.sum(back[:, :TILE], axis=0) for back in (in_back, ctx_back)]
+            total = LEARN_RATE * collect_lent(jnp.concatenate(sums, axis=0), shards)
+            new_in = apply_rows(in_shard, total[:, :TILE].reshape(-1, depth), (asked[0],), (in_back,), (TILE,))
             new_out = new_out.at[:shards * TILE].add(total[:, TILE:].reshape(-1, depth))
             return new_in, new_out
 
         def exchange_full(blocks):
-            return exchange_rows(blocks, 2 + (blocks.shape[1] == full[2]))
+            shapes = (full[0], full[1] - TILE, full[2] - TILE)
+            return exchange_rows(blocks, (2, 3, 6)[shapes.index(blocks.shape[1])])
 
         def branch(swap, caps):
             def call(*args):
@@ -449,7 +467,7 @@
 
             return call
 
-        args = (in_shard, out_shard, lent_in, lent_out, owners, ranks, slots)
+        args = (in_shard, out_shard, lent_in, lent_out, context_ids, negative_ids, owners, ranks, slots)
         return lax.cond(fits, branch(exchange, usual), branch(exchange_full, full), *args)
 
     return jax.shard_map(device_step, mesh=mesh, in_specs=(P(AXIS_NAME, None), P(AXIS_NAME, None), P(AXIS_NAME), P(AXIS_NAME), P(AXIS_NAME)), out_specs=(P(AXIS_NAME, None), P(AXIS_NAME, None)), check_vma=False)

time: 1080 us -> 1120 us (1.037)
  Pallas kernels: 363 us -> 440 us
  waiting for transfers between devices: 421 us -> 352 us
  matrix products: 50.2 us -> 66.9 us
    pallas_call x1, Pallas kernels: 16.8 us -> 93.2 us  [collect_lent(): pl.pallas_call(functools.partial(collect_kernel, shards), out_shape=jax.S...]
    all_to_all x4, waiting for transfers between devices: 421 us -> 352 us  [exchange(): return lax.all_to_all(blocks, AXIS_NAME, 0, 0)]
    dot_general x0 -> x2, matrix products: none -> 17.8 us  [lent_product(): lax.dot_general(a, b, (dims, ((), ())), precision=lax.Precision.HIGHEST)]
  transfers between devices with their start and end apart: 4 -> 4, of which waited for: 4 -> 3; matrix products, arithmetic and copies ran while one was open for 19% -> 15% of each run, Pallas kernels for 0% -> 8%
where the time goes in v3:
time: 1120 us; the launch traced here: 1110 us
  Pallas kernels  440 us (39%)
  waiting for transfers between devices  352 us (31%)
  other arithmetic  134 us (12%)
  local copies, waits for them, and re-layouts  86.3 us (8%)
  matrix products  66.9 us (6%)
  starting transfers between devices  16.9 us (2%)
    all_to_all x4, waiting for transfers between devices, exchange(): return lax.all_to_all(blocks, AXIS_NAME, 0, 0)  352 us
    pallas_call x1, Pallas kernels, fetch_rows(): pl.pallas_call(functools.partial(fetch_kernel, shards), out_shape=(jax.Sh...  260 us
    scatter-add x3, other arithmetic, send_back(): summed = start.reshape(-1, depth).at[cells].add(grads, mode='drop')  97.1 us
    pallas_call x1, Pallas kernels, collect_lent(): pl.pallas_call(functools.partial(collect_kernel, shards), out_shape=jax.S...  93.2 us
    gather x4, local copies, waits for them, and re-layouts, take_rows(): return rows.at[idx].get(mode='promise_in_bounds')  69.8 us
    pallas_call x2, Pallas kernels, apply_rows(): pl.pallas_call(functools.partial(apply_kernel, shards, caps, skips, num_r...  66.8 us
    dot_general x15, matrix products, dot_f32(): lax.dot_general(a, b, (dims, ((), ())), preferred_element_type=jnp.float32)  49 us
  transfers between devices with their start and end apart: 4, of which 3 were waited for; matrix products, arithmetic and copies ran while one was open for 15% of the time, Pallas kernels for 8%

profile of v3, /device:TPU:0, one launch (start us, length us, event | category | flops | bytes accessed | tf_op | source)
XLA Modules:
  0.0 1108.9 jit_solution(18179932776069510823)
XLA Ops:
  4.1 5.5 select_reduce_fusion.1
  15.7 1.6 select_reduce_fusion.2
  18.0 20.2 %ask_owners.1 = (s32[16,8,128]{2,1,0:T(8,128)}, f32[8,2048]{1,0:T(8,128)S(1)}, f32[8,2048]{1,0:T(8,128)S(1)}) custom-call(s32[16,8,128]{2,1,0:T(8,128)} %bitcast.82, f32[2000,2048]{1,0:T(8,128)} %in_shard.1, f32[2000,2048]{1,0:T(8,128)} %out_shard.1), custom_call_target="tpu_custom_call" | custom-call | tf_op jit(solution)/shard_map/ask_owners/pallas_call | solution.py:126
  42.3 1065.5 %conditional.1 = (f32[2000,2048]{1,0:T(8,128)}, f32[2000,2048]{1,0:T(8,128)}) conditional(s32[]{:T(128)} %convert_element_type.182, (s32[16,1024]{1,0:T(8,128)S(1)}, s32[2048]{0:T(1024)S(1)}, s32[2048]{0:T(1024)S(1)}, s32[16,1024]{1,0:T(8,128)S(1)}, s32[16,1024]{1,0:T(8,128)S(1)}, /*index=5*/f32[2000,2048]{1,0:T(8,128)}, f32[8,2048]{1,0:T(8,128)S(1)}, ...), branch_computations={%region_17.24_spmd, %region_24.31_spmd} | conditional | flops 36842991616 | bytes 749580544 | solution.py:471
  51.8 14.5 %gather_fusion.4 = f32[1024,2048]{1,0:T(8,128)} fusion(f32[2000,2048]{1,0:T(8,128)} %get-tuple-element.108.out_shard.refs_3_, s32[1024]{0:T(1024)S(1)} %broadcast_clamp_fusion.2), kind=kCustom, calls=%fused_computation.4 | custom fusion | bytes 16781312 | tf_op jit(solution)/shard_map/cond/branch_1_fun/gather | solution.py:69
  67.4 259.7 %branch_1_fun.1 = (f32[16,64,2048]{2,1,0:T(8,128)S(1)}, f32[16,112,2048]{2,1,0:T(8,128)}, f32[16,112,2048]{2,1,0:T(8,128)}, f32[16,104,2048]{2,1,0:T(8,128)}) custom-call(s32[1792]{0:T(1024)S(1)} %reshape.202.in_idx, s32[1664]{0:T(1024)S(1)} %reshape.203.ctx_idx, f32[16,64,2048]{2,1,0:T(8,128)} %broadcast_dynamic-update-slice_fusion.1.neg_blocks, ...), custom_call_target="tpu_custom_call" | custom-call | tf_op jit(solution)/shard_map/cond/branch_1_fun/pallas_call | solution.py:253
  327.0 3.4 copy-done
  330.4 3.8 all-to-all-start
  334.9 21.7 %gather_fusion.5 = f32[2048,2048]{1,0:T(8,128)} fusion(f32[1792,2048]{1,0:T(8,128)} %bitcast.59, s32[2048]{0:T(1024)S(1)} %get-tuple-element.167), kind=kCustom, calls=%fused_computation.5 | custom fusion | bytes 33562624 | tf_op jit(solution)/shard_map/cond/branch_1_fun/gather | solution.py:69
  357.2 12.2 %gather_fusion.6 = bf16[1024,2048]{1,0:T(8,128)(2,1)} fusion(f32[1024,2048]{1,0:T(8,128)} %bitcast.58, s32[1024]{0:T(1024)S(1)} %get-tuple-element.166), kind=kCustom, calls=%fused_computation.6 | custom fusion | bytes 8392704 | tf_op jit(solution)/shard_map/cond/branch_1_fun/gather | solution.py:69
  369.4 11.1 %fusion.57 = f32[2048,2048]{1,0:T(8,128)} fusion(f32[16,64,2048]{2,1,0:T(8,128)} %copy-done, s32[2048]{0:T(1024)S(1)} %get-tuple-element.115), kind=kOutput, calls=%fused_computation.102 | convolution fusion | flops 6442713088 | bytes 17833984 | tf_op jit(solution)/shard_map/cond/branch_1_fun/dot_general | solution.py:410
  380.5 15.9 %multiply_convert_fusion.1 = bf16[2048,1024]{1,0:T(8,128)(2,1)} fusion(f32[2048,2048]{1,0:T(8,128)} %gather_fusion.5, bf16[1024,2048]{1,0:T(8,128)(2,1)} %gather_fusion.6), kind=kOutput, calls=%fused_computation.83 | convolution fusion | flops 8604614656 | bytes 25165824 | tf_op jit(solution)/shard_map/cond/branch_1_fun/dot_general | solution.py:33
  396.4 15.4 %fusion.127 = f32[2048,2048]{1,0:T(8,128)} fusion(bf16[2048,1024]{1,0:T(8,128)(2,1)} %multiply_convert_fusion.1, bf16[1024,2048]{1,0:T(8,128)(2,1)} %gather_fusion.6), kind=kOutput, calls=%fused_computation.279 | convolution fusion | flops 8589934592 | bytes 25165824 | tf_op jit(solution)/shard_map/cond/branch_1_fun/dot_general | solution.py:33
  411.9 13.1 %fusion.46 = f32[1024,2048]{1,0:T(8,128)} fusion(bf16[2048,1024]{1,0:T(8,128)(2,1)} %multiply_convert_fusion.1, f32[2048,2048]{1,0:T(8,128)S(1)} %bitcast.63), kind=kOutput, calls=%fused_computation.90 | convolution fusion | flops 8594128896 | bytes 29360128 | tf_op jit(solution)/shard_map/cond/branch_1_fun/dot_general | solution.py:33
  425.1 6.8 fusion.50
  431.8 7.3 pad.14
  439.2 58.1 %all-to-all-done = f32[16,104,2048]{2,1,0:T(8,128)} async-done(((f32[16,104,2048]{2,1,0:T(8,128)}), f32[16,104,2048]{2,1,0:T(8,128)}, u32[]{:S(2)}, u32[]{:S(2)}) %all-to-all-start) | async-done | bytes 13631520 | tf_op jit(solution)/shard_map/cond/branch_1_fun/all_to_all | solution.py:65
  497.2 21.4 %gather_fusion.7 = f32[2048,2048]{1,0:T(8,128)} fusion(f32[1664,2048]{1,0:T(8,128)} %bitcast.16, s32[2048]{0:T(1024)S(1)} %get-tuple-element.163), kind=kCustom, calls=%fused_computation.7 | custom fusion | bytes 33562624 | tf_op jit(solution)/shard_map/cond/branch_1_fun/gather | solution.py:69
  518.6 16.5 %multiply_reduce_fusion.1 = f32[2048]{0:T(1024)S(1)} fusion(f32[2048,2048]{1,0:T(8,128)} %gather_fusion.5, f32[2048,2048]{1,0:T(8,128)} %fusion.57, f32[2048,2048]{1,0:T(8,128)} %gather_fusion.7, pred[2048]{0:T(1024)(128)(4,1)S(1)} %broadcast_compare_fusion.1), kind=kLoop, calls=%fused_computation.80 | loop fusion | flops 12580864 | bytes 50341888 | tf_op jit(solution)/shard_map/cond/branch_1_fun/reduce_sum | solution.py:448
  535.1 39.4 %scatter_custom_fusion.4 = f32[1792,2048]{1,0:T(8,128)} fusion(f32[1792,2048]{1,0:T(8,128)} %bitcast.69, s32[2048]{0:T(1024)} %get-tuple-element.164, f32[2048,2048]{1,0:T(8,128)} %gather_fusion.5, f32[2048]{0:T(1024)S(1)} %divide_add_fusion.1), kind=kCustom, calls=%fused_computation.73 | custom fusion | flops 12582912 | bytes 31465472 | tf_op jit(solution)/shard_map/cond/branch_1_fun/scatter-add | solution.py:420
  574.5 4.6 all-to-all-start.2
  579.1 39.0 %scatter_custom_fusion.3 = f32[1792,2048]{1,0:T(8,128)} fusion(s32[2048]{0:T(1024)} %get-tuple-element.168, f32[2048,2048]{1,0:T(8,128)} %fusion.127, f32[2048]{0:T(1024)S(1)} %divide_add_fusion.1, f32[]{:T(128)} %constant.306.clone, f32[2048,2048]{1,0:T(8,128)} %fusion.57, f32[2048,2048]{1,0:T(8,128)} %gather_fusion.7, ...), kind=kCustom, calls=%fused_computation.76 | custom fusion | flops 20971520 | bytes 65022464 | tf_op jit(solution)/shard_map/cond/branch_1_fun/scatter-add | solution.py:420
  618.1 136.6 %all-to-all-done.2.refs_5_ = f32[16,112,2048]{2,1,0:T(8,128)} async-done(((f32[16,112,2048]{2,1,0:T(8,128)}), f32[16,112,2048]{2,1,0:T(8,128)}, u32[]{:S(2)}, u32[]{:S(2)}) %all-to-all-start.2) | async-done | bytes 14680096 | tf_op jit(solution)/shard_map/cond/branch_1_fun/all_to_all | solution.py:65
  754.7 4.3 all-to-all-start.1
  759.0 18.7 %scatter_custom_fusion.5 = f32[896,2048]{1,0:T(8,128)} fusion(s32[1024]{0:T(1024)} %get-tuple-element.165, f32[1024,2048]{1,0:T(8,128)} %fusion.46, f32[]{:T(128)} %constant.306.clone), kind=kCustom, calls=%fused_computation.85 | custom fusion | flops 4194304 | bytes 15729152 | tf_op jit(solution)/shard_map/cond/branch_1_fun/scatter-add | solution.py:420
  777.7 156.9 %all-to-all-done.1.refs_3_ = f32[16,112,2048]{2,1,0:T(8,128)} async-done(((f32[16,112,2048]{2,1,0:T(8,128)}), f32[16,112,2048]{2,1,0:T(8,128)}, u32[]{:S(2)}, u32[]{:S(2)}) %all-to-all-start.1) | async-done | bytes 14680096 | tf_op jit(solution)/shard_map/cond/branch_1_fun/all_to_all | solution.py:65
  934.7 4.1 all-to-all-start.3
  943.8 93.2 %collect_lent.3 = f32[16,16,2048]{2,1,0:T(8,128)} custom-call(f32[16,2048]{1,0:T(8,128)} %pad_maximum_fusion.1.mine), custom_call_target="tpu_custom_call" | custom-call | tf_op jit(solution)/shard_map/cond/branch_1_fun/collect_lent/pallas_call | solution.py:287
  1037.0 1.3 slice_bitcast_fusion.1.refs_1_
  1038.4 39.3 %apply_rows.7 = f32[2000,2048]{1,0:T(8,128)} custom-call(s32[896]{0:T(1024)S(1)} %reshape.213.refs_0_, s32[1792]{0:T(1024)S(1)} %reshape.214.refs_1_, f32[8,2048]{1,0:T(8,128)S(1)} %broadcast_93_refs_2_.0.refs_2_, f32[2000,2048]{1,0:T(8,128)} %get-tuple-element.108.out_shard.refs_3_, f32[16,56,2048]{2,1,0:T(8,128)} %all-to-all-done.3.refs_4_, ...), custom_call_target="tpu_custom_call" | custom-call | flops 547880960 | bytes 54788096 | tf_op jit(solution)/shard_map/cond/branch_1_fun/apply_rows/pallas_call | solution.py:373
  1077.7 2.3 fusion.56
  1080.0 27.5 %apply_rows.6 = f32[2000,2048]{1,0:T(8,128)} custom-call(s32[1792]{0:T(1024)S(1)} %reshape.201.refs_0_, f32[128,2048]{1,0:T(8,128)S(1)} %slice_bitcast_fusion.1.refs_1_, f32[2000,2048]{1,0:T(8,128)} %get-tuple-element.111.in_shard.refs_2_, f32[16,112,2048]{2,1,0:T(8,128)} %all-to-all-done.1.refs_3_), custom_call_target="tpu_custom_call" | custom-call | flops 474480640 | bytes 47448064 | tf_op jit(solution)/shard_map/cond/branch_1_fun/apply_rows/pallas_call | solution.py:373
  (104 shorter events, 20.5 us)
Async XLA Ops:
  18.0 23.0 %copy-start.19 = (s32[3]{0:T(128)S(1)}, s32[3]{0:T(128)}, u32[]{:S(2)}) copy-start(s32[3]{0:T(128)} %constant.334.clone) | copy-start | bytes 40
  18.0 23.6 %copy-start.7 = (s32[2048]{0:T(1024)S(1)}, s32[2048]{0:T(1024)}, u32[]{:S(2)}) copy-start(s32[2048]{0:T(1024)} %param.15) | copy-start | bytes 24580
  50.2 0.6 copy-start.16
  50.3 16.0 %copy-start.6 = (s32[16,1024]{1,0:T(8,128)}, s32[16,1024]{1,0:T(8,128)S(1)}, u32[]{:S(2)}) copy-start(s32[16,1024]{1,0:T(8,128)S(1)} %get-tuple-element.139) | copy-start | bytes 196612 | tf_op jit(solution)/shard_map/cond
  50.3 284.0 %copy-start.10 = (s32[2048]{0:T(1024)}, s32[2048]{0:T(1024)S(1)}, u32[]{:S(2)}) copy-start(s32[2048]{0:T(1024)S(1)} %get-tuple-element.114) | copy-start | bytes 24580 | tf_op jit(solution)/shard_map/cond
  327.0 3.4 copy-start
  330.4 166.8 %all-to-all-start = ((f32[16,104,2048]{2,1,0:T(8,128)}), f32[16,104,2048]{2,1,0:T(8,128)}, u32[]{:S(2)}, u32[]{:S(2)}) async-start(f32[16,104,2048]{2,1,0:T(8,128)} %get-tuple-element.120), calls=%async_computation | async-start | bytes 27262976 | tf_op jit(solution)/shard_map/cond/branch_1_fun/all_to_all | solution.py:65
  334.9 21.7 %copy-start.17 = (s32[1024]{0:T(1024)S(1)}, s32[1024]{0:T(1024)}, u32[]{:S(2)}) copy-start(s32[1024]{0:T(1024)} %copy-done.16) | copy-start | bytes 12292 | tf_op jit(solution)/shard_map/cond
  380.5 31.4 %slice-start = ((s8[16777216]{0:T(1024)(128)(4,1)}), s8[4194304]{0:T(1024)(128)(4,1)S(1)}, s32[]{:S(2)}) async-start(s8[16777216]{0:T(1024)(128)(4,1)} %bitcast.62), calls=%async_computation.4 | async-start | bytes 8388608 | tf_op jit(solution)/shard_map/cond
  380.5 31.4 %slice-start.1 = ((s8[16777216]{0:T(1024)(128)(4,1)}), s8[4194304]{0:T(1024)(128)(4,1)S(1)}, s32[]{:S(2)}) async-start(s8[16777216]{0:T(1024)(128)(4,1)} %bitcast.62), calls=%async_computation.5 | async-start | bytes 8388608 | tf_op jit(solution)/shard_map/cond
  380.5 31.4 %slice-start.2 = ((s8[16777216]{0:T(1024)(128)(4,1)}), s8[4194304]{0:T(1024)(128)(4,1)S(1)}, s32[]{:S(2)}) async-start(s8[16777216]{0:T(1024)(128)(4,1)} %bitcast.62), calls=%async_computation.6 | async-start | bytes 8388608 | tf_op jit(solution)/shard_map/cond
  396.4 15.5 %slice-start.3 = ((s8[16777216]{0:T(1024)(128)(4,1)}), s8[4194304]{0:T(1024)(128)(4,1)S(1)}, s32[]{:S(2)}) async-start(s8[16777216]{0:T(1024)(128)(4,1)} %bitcast.62), calls=%async_computation.7 | async-start | bytes 8388608 | tf_op jit(solution)/shard_map/cond
  411.9 13.1 %copy-start.15 = (s32[1024]{0:T(1024)S(1)}, s32[1024]{0:T(1024)}, u32[]{:S(2)}) copy-start(s32[1024]{0:T(1024)} %get-tuple-element.123) | copy-start | bytes 12292 | tf_op jit(solution)/shard_map/cond
  425.0 14.1 %copy-start.11 = (s32[2048]{0:T(1024)S(1)}, s32[2048]{0:T(1024)}, u32[]{:S(2)}) copy-start(s32[2048]{0:T(1024)} %copy-done.10) | copy-start | bytes 24580 | tf_op jit(solution)/shard_map/cond
  574.5 180.2 %all-to-all-start.2 = ((f32[16,112,2048]{2,1,0:T(8,128)}), f32[16,112,2048]{2,1,0:T(8,128)}, u32[]{:S(2)}, u32[]{:S(2)}) async-start(f32[16,112,2048]{2,1,0:T(8,128)} %bitcast.70), calls=%async_computation.2 | async-start | bytes 29360128 | tf_op jit(solution)/shard_map/cond/branch_1_fun/all_to_all | solution.py:65
  754.7 180.0 %all-to-all-start.1 = ((f32[16,112,2048]{2,1,0:T(8,128)}), f32[16,112,2048]{2,1,0:T(8,128)}, u32[]{:S(2)}, u32[]{:S(2)}) async-start(f32[16,112,2048]{2,1,0:T(8,128)} %bitcast.71), calls=%async_computation.1 | async-start | bytes 29360128 | tf_op jit(solution)/shard_map/cond/branch_1_fun/all_to_all | solution.py:65
  759.0 181.5 %copy-start.18 = (s32[16,112]{1,0:T(8,128)S(1)}, s32[16,112]{1,0:T(8,128)}, u32[]{:S(2)}) copy-start(s32[16,112]{1,0:T(8,128)} %get-tuple-element.162) | copy-start | bytes 21508 | tf_op jit(solution)/shard_map/cond
  934.7 103.7 %all-to-all-start.3 = ((f32[16,56,2048]{2,1,0:T(8,128)}), f32[16,56,2048]{2,1,0:T(8,128)}, u32[]{:S(2)}, u32[]{:S(2)}) async-start(f32[16,56,2048]{2,1,0:T(8,128)} %bitcast.74), calls=%async_computation.3 | async-start | bytes 14680064 | tf_op jit(solution)/shard_map/cond/branch_1_fun/all_to_all | solution.py:65
  1038.4 39.3 %copy-start.3 = (f32[16,16,2048]{2,1,0:T(8,128)S(1)}, f32[16,16,2048]{2,1,0:T(8,128)}, u32[]{:S(2)}) copy-start(f32[16,16,2048]{2,1,0:T(8,128)} %collect_lent.3) | copy-start | bytes 6291460 | tf_op jit(solution)/shard_map/cond

commit v4 on v3

--- a/solution.py
+++ b/solution.py
@@ -52,13 +52,12 @@
     before = (lax.broadcasted_iota(jnp.int32, (SLOT_BLOCKS, SLOT_BLOCKS), 0) < lax.broadcasted_iota(jnp.int32, (SLOT_BLOCKS, SLOT_BLOCKS), 1))
     block_start = dot_f32(block_total.astype(jnp.bfloat16), before.astype(jnp.bfloat16), ((1,), (0,)))
     rank = inclusive - ones.astype(jnp.float32) + block_start.reshape(-1)[:, None]
-    largest = jnp.max(jnp.sum(block_total, axis=1)).astype(jnp.int32)
     rank_of_id = jnp.sum(dot_f32(high, rank.astype(jnp.bfloat16), ((1,), (0,))) * low.astype(jnp.float32), axis=1).astype(jnp.int32)
     rank_or_none = jnp.where(present, rank, -1.0).reshape(shards, 1, SLOT_BLOCKS * LANES)
     cells = lax.broadcasted_iota(jnp.int32, (1, capacity, 1), 1).astype(jnp.float32)
     slots = lax.broadcasted_iota(jnp.int32, (1, 1, SLOT_BLOCKS * LANES), 2).astype(jnp.float32)
     slot_of_cell = jnp.sum(jnp.where(rank_or_none == cells, slots + 1.0, 0.0), axis=2).astype(jnp.int32) - 1
-    return owner, rank_of_id, slot_of_cell, largest
+    return owner, rank_of_id, slot_of_cell
 
 
 def exchange(blocks):
@@ -80,58 +79,31 @@
     return pltpu.make_async_remote_copy(src_ref=src, dst_ref=dst, send_sem=send_sem, recv_sem=recv_sem, device_id=(peer,), device_id_type=pl.DeviceIdType.MESH)
 
 
-def ask_kernel(shards, ask, in_shard, out_shard, got, lent_in, lent_out, ask_send, ask_recv, lend_send, lend_recv, own_sem):
+def ask_kernel(shards, ask, got, send_sem, recv_sem):
     me = lax.axis_index(AXIS_NAME)
     meet(me, shards)
-
-    def lend(peer, part):
-        table, lent = ((in_shard, lent_in), (out_shard, lent_out))[part]
-        return remote(table.at[pl.ds(pl.multiple_of(peer * TILE, TILE), TILE)], lent, lend_send.at[part, peer], lend_recv.at[part], peer)
-
-    @pl.when(me == 0)
-    def _():
-        for peer in range(1, shards):
-            lend(peer, 0).start()
-            lend(peer, 1).start()
-        pltpu.make_async_copy(in_shard.at[pl.ds(0, TILE)], lent_in, own_sem.at[0]).start()
-        pltpu.make_async_copy(out_shard.at[pl.ds(0, TILE)], lent_out, own_sem.at[1]).start()
-
     copies = []
     for step in range(1, shards):
         peer = lax.rem(me + step, shards)
-        copies.append(remote(ask.at[peer], got.at[me], ask_send.at[step], ask_recv.at[step], peer))
+        copies.append(remote(ask.at[peer], got.at[me], send_sem.at[step], recv_sem.at[step], peer))
         copies[-1].start()
     got[me] = ask[me]
     for copy in copies:
         copy.wait()
 
-    @pl.when(me == 0)
-    def _():
-        for peer in range(1, shards):
-            lend(peer, 0).wait_send()
-            lend(peer, 1).wait_send()
-        pltpu.make_async_copy(in_shard.at[pl.ds(0, TILE)], lent_in, own_sem.at[0]).wait()
-        pltpu.make_async_copy(out_shard.at[pl.ds(0, TILE)], lent_out, own_sem.at[1]).wait()
-
-    @pl.when(me != 0)
-    def _():
-        lend(me, 0).wait_recv()
-        lend(me, 1).wait_recv()
-
-
-def ask_owners(ask, in_shard, out_shard, shards):
-    depth = in_shard.shape[1]
-    any_space, vmem = pl.BlockSpec(memory_space=pl.ANY), pl.BlockSpec(memory_space=pltpu.VMEM)
-    tile = jax.ShapeDtypeStruct((TILE, depth), jnp.float32)
+
+def ask_owners(ask):
+    shards = ask.shape[0]
+    vmem = pl.BlockSpec(memory_space=pltpu.VMEM)
     return pl.pallas_call(
         functools.partial(ask_kernel, shards),
-        out_shape=(jax.ShapeDtypeStruct(ask.shape, jnp.int32), tile, tile),
-        in_specs=[vmem, any_space, any_space],
-        out_specs=(vmem, vmem, vmem),
-        scratch_shapes=[pltpu.SemaphoreType.DMA((shards,)), pltpu.SemaphoreType.DMA((shards,)), pltpu.SemaphoreType.DMA((2, shards)), pltpu.SemaphoreType.DMA((2,)), pltpu.SemaphoreType.DMA((2,))],
+        out_shape=jax.ShapeDtypeStruct(ask.shape, jnp.int32),
+        in_specs=[vmem],
+        out_specs=vmem,
+        scratch_shapes=[pltpu.SemaphoreType.DMA((shards,)), pltpu.SemaphoreType.DMA((shards,))],
         compiler_params=pltpu.CompilerParams(collective_id=0, has_side_effects=True),
         name='ask_owners',
-    )(ask, in_shard, out_shard)
+    )(ask)
 
 
 def exchange_kernel(shards, blocks, got, send_sem, recv_sem, own_sem):
@@ -169,33 +141,47 @@
     )(blocks)
 
 
-def fetch_kernel(shards, in_idx, ctx_idx, neg_blocks, in_shard, out_shard, lent_in, neg_got, in_got, in_blocks, ctx_blocks,
-                 held, stage, neg_send, neg_recv, in_send, in_recv, own_sem, load_sem, stage_sem):
+def fetch_kernel(shards, in_idx, ctx_idx, neg_blocks, in_shard, out_shard, neg_got, in_got, in_blocks, ctx_blocks,
+                 held, stage, lent, neg_send, neg_recv, in_send, in_recv, hot_send, hot_recv, lend_send, lend_recv, own_sem, load_sem, stage_sem):
     me = lax.axis_index(AXIS_NAME)
     load_in = pltpu.make_async_copy(in_shard, held, load_sem)
     load_in.start()
     meet(me, shards)
 
+    def lend(part, peer):
+        table = (in_shard, out_shard)[part]
+        return remote(table.at[pl.ds(pl.multiple_of(peer * TILE, TILE), TILE)], lent.at[part], lend_send.at[part, peer], lend_recv.at[part], peer)
+
+    def keep(part):
+        return pltpu.make_async_copy((in_shard, out_shard)[part].at[pl.ds(0, TILE)], lent.at[part], own_sem.at[2 + part])
+
+    @pl.when(me == 0)
+    def _():
+        for part in range(2):
+            keep(part).start()
+            for peer in range(1, shards):
+                lend(part, peer).start()
+
     def exchange(blocks, got, send_sem, recv_sem):
         count = blocks.shape[1]
 
-        def copy(step, rows):
+        def copy(step, first, rows):
             peer = lax.rem(me + step, shards)
-            return remote(blocks.at[peer, rows], got.at[me, rows], send_sem.at[step], recv_sem.at[step], peer)
+            return remote(blocks.at[peer, pl.ds(first, rows)], got.at[me, pl.ds(first + TILE, rows)], send_sem.at[step], recv_sem.at[step], peer)
 
         def send(tile, carry):
             for step in range(1, shards):
-                copy(step, pl.ds(pl.multiple_of(tile * TILE, TILE), TILE)).start()
+                copy(step, pl.multiple_of(tile * TILE, TILE), TILE).start()
             return carry
 
         def finish():
             for step in range(1, shards):
-                copy(step, pl.ds(0, count)).wait()
+                copy(step, 0, count).wait()
 
         lax.fori_loop(0, count // TILE, send, 0)
         return finish
 
-    def pick(idx, lent, blocks):
+    def pick(idx, blocks):
         count = blocks.shape[1]
 
         def put(peer, place):
@@ -207,9 +193,6 @@
             @pl.when(peer >= 2)
             def _():
                 put(peer - 2, place).wait()
-
-            if lent is not None:
-                stage[place, pl.ds(0, TILE), :] = lent[...]
 
             def group(step, carry):
                 first = step * TILE
@@ -217,7 +200,7 @@
                     stage[place, pl.ds(first + k, 1), :] = held[pl.ds(idx[peer * count + first + k], 1), :]
                 return carry
 
-            lax.fori_loop(0 if lent is None else 1, count // TILE, group, 0)
+            lax.fori_loop(0, count // TILE, group, 0)
             put(peer, place).start()
             return carry
 
@@ -226,38 +209,65 @@
         put(shards - 1, 1).wait()
 
     finish_neg = exchange(neg_blocks, neg_got, neg_send, neg_recv)
-    own_neg = pltpu.make_async_copy(neg_blocks.at[me], neg_got.at[me], own_sem.at[0])
+    own_neg = pltpu.make_async_copy(neg_blocks.at[me], neg_got.at[me, pl.ds(TILE, neg_blocks.shape[1])], own_sem.at[0])
     own_neg.start()
     load_in.wait()
-    pick(in_idx, lent_in, in_blocks)
+    pick(in_idx, in_blocks)
+
+    @pl.when(me == 0)
+    def _():
+        for part in range(2):
+            keep(part).wait()
+            for peer in range(1, shards):
+                lend(part, peer).wait_send()
+
+    @pl.when(me != 0)
+    def _():
+        for part in range(2):
+            lend(part, me).wait_recv()
+
+    hot = []
+    for part, got in enumerate((in_got, neg_got)):
+        hot.append(pltpu.make_async_copy(lent.at[part], got.at[me, pl.ds(0, TILE)], own_sem.at[4 + part]))
+        for step in range(1, shards):
+            hot.append(remote(lent.at[part], got.at[me, pl.ds(0, TILE)], hot_send.at[part, step], hot_recv.at[part, step], lax.rem(me + step, shards)))
+    for copy in hot:
+        copy.start()
     finish_in = exchange(in_blocks, in_got, in_send, in_recv)
-    own_in = pltpu.make_async_copy(in_blocks.at[me], in_got.at[me], own_sem.at[1])
+    own_in = pltpu.make_async_copy(in_blocks.at[me], in_got.at[me, pl.ds(TILE, in_blocks.shape[1])], own_sem.at[1])
     own_in.start()
     load_out = pltpu.make_async_copy(out_shard, held, load_sem)
     load_out.start()
     load_out.wait()
-    pick(ctx_idx, None, ctx_blocks)
+    pick(ctx_idx, ctx_blocks)
     own_neg.wait()
     own_in.wait()
     finish_neg()
+    for copy in hot:
+        copy.wait()
     finish_in()
 
 
-def fetch_rows(in_slot, ctx_slot, neg_blocks, in_shard, out_shard, lent_in, collective_id):
+def fetch_rows(in_slot, ctx_slot, neg_blocks, in_shard, out_shard, collective_id):
     shards, in_cap = in_slot.shape
     ctx_cap, depth = ctx_slot.shape[1], in_shard.shape[1]
-    smem, vmem, any_space = (pl.BlockSpec(memory_space=space) for space in (pltpu.SMEM, pltpu.VMEM, pl.ANY))
-    in_shape = jax.ShapeDtypeStruct((shards, in_cap, depth), jnp.float32)
-    ctx_shape = jax.ShapeDtypeStruct((shards, ctx_cap, depth), jnp.float32)
-    sems = pltpu.SemaphoreType.DMA((shards,))
+    smem, any_space = pl.BlockSpec(memory_space=pltpu.SMEM), pl.BlockSpec(memory_space=pl.ANY)
+
+    def rows(count):
+        return jax.ShapeDtypeStruct((shards, count, depth), jnp.float32)
+
+    def sems(*shape):
+        return pltpu.SemaphoreType.DMA(shape)
+
     neg_got, in_got, _, ctx_blocks = pl.pallas_call(
         functools.partial(fetch_kernel, shards),
-        out_shape=(jax.ShapeDtypeStruct(neg_blocks.shape, jnp.float32), in_shape, in_shape, ctx_shape),
-        in_specs=[smem, smem, any_space, any_space, any_space, vmem],
+        out_shape=(rows(neg_blocks.shape[1] + TILE), rows(in_cap + TILE), rows(in_cap), rows(ctx_cap)),
+        in_specs=[smem, smem, any_space, any_space, any_space],
         out_specs=(any_space,) * 4,
-        scratch_shapes=[pltpu.VMEM(in_shard.shape, jnp.float32), pltpu.VMEM((2, max(in_cap, ctx_cap), depth), jnp.float32), sems, sems, sems, sems, pltpu.SemaphoreType.DMA((2,)), pltpu.SemaphoreType.DMA, pltpu.SemaphoreType.DMA((2,))],
+        scratch_shapes=[pltpu.VMEM(in_shard.shape, jnp.float32), pltpu.VMEM((2, max(in_cap, ctx_cap), depth), jnp.float32), pltpu.VMEM((2, TILE, depth), jnp.float32)]
+        + [sems(shards)] * 4 + [sems(2, shards)] * 3 + [sems(2), sems(6), pltpu.SemaphoreType.DMA, sems(2)],
         compiler_params=pltpu.CompilerParams(collective_id=collective_id, has_side_effects=True, vmem_limit_bytes=40 * 2**20),
-    )(jnp.maximum(in_slot - TILE, 0).reshape(-1), jnp.maximum(ctx_slot - TILE, 0).reshape(-1), neg_blocks, in_shard, out_shard, lent_in)
+    )(jnp.maximum(in_slot - TILE, 0).reshape(-1), jnp.maximum(ctx_slot - TILE, 0).reshape(-1), neg_blocks, in_shard, out_shard)
     return neg_got.reshape(-1, depth), in_got.reshape(-1, depth), ctx_blocks
 
 
@@ -392,16 +402,16 @@
         full = tuple(up8(distinct_bound(ids.shape[0], shards) + TILE) for ids in lists)
         usual = tuple(up8(TILE + ids.shape[0] * 13 // (16 * shards)) for ids in lists)
 
-        owners, ranks, asks, largest = zip(*(request_layout(ids, shard_rows, shards, cap) for ids, cap in zip(lists, full)))
-        counts = jnp.broadcast_to(jnp.stack(largest)[None, :], (shards, 3))
-        ask = jnp.concatenate(asks + (counts,), axis=1)
+        owners, ranks, asks = zip(*(request_layout(ids, shard_rows, shards, cap) for ids, cap in zip(lists, full)))
+        beyond = jnp.concatenate([ask[:, cap:cap + 1] for ask, cap in zip(asks, usual)], axis=1)
+        over = jnp.broadcast_to(jnp.max(beyond), (shards, 1))
+        ask = jnp.concatenate(asks + (over,), axis=1)
         ask = jnp.pad(ask, ((0, 0), (0, HEADER * LANES - ask.shape[1]))).reshape(shards, HEADER, LANES)
-        arrived, lent_in, lent_out = ask_owners(ask, in_shard, out_shard, shards)
+        arrived = ask_owners(ask)
         arrived = arrived.reshape(shards, HEADER * LANES)
         edge1, edge2, edge3 = full[0], full[0] + full[1], sum(full)
         slots = (arrived[:, :edge1], arrived[:, edge1:edge2], arrived[:, edge2:edge3])
-        most = jnp.max(arrived[:, edge3:edge3 + 3], axis=0)
-        fits = jnp.all(most <= jnp.array(usual, jnp.int32))
+        fits = jnp.max(arrived[:, edge3]) < 0
 
         def onehot_f32(ids):
             return (ids[:, None] == lax.broadcasted_iota(jnp.int32, (1, shards * TILE), 1)).astype(jnp.float32)
@@ -409,12 +419,8 @@
         def lent_product(a, b, dims):
             return lax.dot_general(a, b, (dims, ((), ())), precision=lax.Precision.HIGHEST)
 
-        def run(exchange, caps, in_shard, out_shard, lent_in, lent_out, context_ids, negative_ids, owners, ranks, slots):
+        def run(exchange, caps, in_shard, out_shard, context_ids, negative_ids, owners, ranks, slots):
             asked = [slot[:, :cap] for slot, cap in zip(slots, caps)]
-
-            def pick(table, lent, slot):
-                rows = take_rows(table, jnp.maximum(slot - TILE, 0))
-                return lax.dynamic_update_slice(rows, jnp.broadcast_to(lent[None], (shards, TILE, depth)), (0, 0, 0))
 
             def send_back(start, cells, grads):
                 summed = start.reshape(-1, depth).at[cells].add(grads, mode='drop')
@@ -427,8 +433,8 @@
             neg_cell = owners[2] * neg_cap + ranks[2]
             neg_cold = jnp.where(ranks[2] < TILE, shards * (neg_cap - TILE), neg_cell - TILE * (owners[2] + 1))
 
-            picked = pick(out_shard, lent_out, asked[2])
-            neg_rows, in_rows, ctx_blocks = fetch_rows(asked[0], asked[1][:, TILE:], picked, in_shard, out_shard, lent_in, 4 if caps == usual else 5)
+            picked = take_rows(out_shard, jnp.maximum(asked[2][:, TILE:] - TILE, 0))
+            neg_rows, in_rows, ctx_blocks = fetch_rows(asked[0][:, TILE:], asked[1][:, TILE:], picked, in_shard, out_shard, 4 if caps == usual else 5)
             ctx_rows = exchange(ctx_blocks).reshape(-1, depth)
 
             negative_half = take_rows(neg_rows, neg_cell).astype(jnp.bfloat16)
@@ -467,7 +473,7 @@
 
             return call
 
-        args = (in_shard, out_shard, lent_in, lent_out, context_ids, negative_ids, owners, ranks, slots)
+        args = (in_shard, out_shard, context_ids, negative_ids, owners, ranks, slots)
         return lax.cond(fits, branch(exchange, usual), branch(exchange_full, full), *args)
 
     return jax.shard_map(device_step, mesh=mesh, in_specs=(P(AXIS_NAME, None), P(AXIS_NAME, None), P(AXIS_NAME), P(AXIS_NAME), P(AXIS_NAME)), out_specs=(P(AXIS_NAME, None), P(AXIS_NAME, None)), check_vma=False)

time: 1120 us -> 1120 us (level)
  no operation moved by 1% of the time
where the time goes in v4:
time: 1120 us; the launch traced here: 1110 us
  Pallas kernels  440 us (39%)
  waiting for transfers between devices  352 us (31%)
  other arithmetic  134 us (12%)
  local copies, waits for them, and re-layouts  84.2 us (8%)
  matrix products  66.9 us (6%)
  starting transfers between devices  16.9 us (2%)
    all_to_all x4, waiting for transfers between devices, exchange(): return lax.all_to_all(blocks, AXIS_NAME, 0, 0)  352 us
    pallas_call x1, Pallas kernels, fetch_rows(): pl.pallas_call(functools.partial(fetch_kernel, shards), out_shape=(rows(n...  270 us
    scatter-add x3, other arithmetic, send_back(): summed = start.reshape(-1, depth).at[cells].add(grads, mode='drop')  97.1 us
    pallas_call x1, Pallas kernels, collect_lent(): pl.pallas_call(functools.partial(collect_kernel, shards), out_shape=jax.S...  93.3 us
    gather x4, local copies, waits for them, and re-layouts, take_rows(): return rows.at[idx].get(mode='promise_in_bounds')  69.5 us
    pallas_call x2, Pallas kernels, apply_rows(): pl.pallas_call(functools.partial(apply_kernel, shards, caps, skips, num_r...  66.8 us
    dot_general x15, matrix products, dot_f32(): lax.dot_general(a, b, (dims, ((), ())), preferred_element_type=jnp.float32)  49 us
  transfers between devices with their start and end apart: 4, of which 3 were waited for; matrix products, arithmetic and copies ran while one was open for 15% of the time, Pallas kernels for 8%

profile of v4, /device:TPU:0, one launch (start us, length us, event | category | flops | bytes accessed | tf_op | source)
XLA Modules:
  0.0 1107.2 jit_solution(301508424853581714)
XLA Ops:
  4.1 5.5 select_reduce_fusion.1
  14.1 1.6 select_reduce_fusion.2
  17.9 9.3 ask_owners.1
  31.3 1074.8 %conditional.1 = (f32[2000,2048]{1,0:T(8,128)}, f32[2000,2048]{1,0:T(8,128)}) conditional(s32[]{:T(128)} %convert_element_type.182, (s32[16,1024]{1,0:T(8,128)S(1)}, s32[2048]{0:T(1024)S(1)}, s32[2048]{0:T(1024)S(1)}, s32[16,1024]{1,0:T(8,128)S(1)}, s32[16,1024]{1,0:T(8,128)S(1)}, /*index=5*/f32[2000,2048]{1,0:T(8,128)}, f32[2000,2048]{1,0:T(8,128)}, ...), branch_computations={%region_13.20_spmd, %region_20.27_spmd} | conditional | flops 36842995712 | bytes 801111872 | solution.py:477
  41.1 14.3 %gather_fusion.4 = f32[896,2048]{1,0:T(8,128)} fusion(f32[2000,2048]{1,0:T(8,128)} %get-tuple-element.127.out_shard.refs_3_, s32[1024]{0:T(1024)S(1)} %pad_clamp_fusion.1), kind=kCustom, calls=%fused_computation.4 | custom fusion | bytes 14683648 | tf_op jit(solution)/shard_map/cond/branch_1_fun/gather | solution.py:68
  55.4 3.1 copy-done.2
  58.4 270.3 %branch_1_fun.1 = (f32[16,64,2048]{2,1,0:T(8,128)}, f32[16,112,2048]{2,1,0:T(8,128)}, f32[16,104,2048]{2,1,0:T(8,128)}, f32[16,104,2048]{2,1,0:T(8,128)}) custom-call(s32[1664]{0:T(1024)S(1)} %reshape.199.in_idx, s32[1664]{0:T(1024)S(1)} %reshape.200.ctx_idx, f32[16,56,2048]{2,1,0:T(8,128)S(1)} %bitcast.60, ...), custom_call_target="tpu_custom_call" | custom-call | tf_op jit(solution)/shard_map/cond/branch_1_fun/pallas_call | solution.py:262
  328.7 3.9 all-to-all-start
  333.2 21.7 %gather_fusion.5 = f32[2048,2048]{1,0:T(8,128)} fusion(f32[1792,2048]{1,0:T(8,128)} %bitcast.61, s32[2048]{0:T(1024)S(1)} %get-tuple-element.162), kind=kCustom, calls=%fused_computation.5 | custom fusion | bytes 33562624 | tf_op jit(solution)/shard_map/cond/branch_1_fun/gather | solution.py:68
  355.5 12.2 %gather_fusion.6 = bf16[1024,2048]{1,0:T(8,128)(2,1)} fusion(f32[1024,2048]{1,0:T(8,128)} %bitcast.66, s32[1024]{0:T(1024)S(1)} %get-tuple-element.159), kind=kCustom, calls=%fused_computation.6 | custom fusion | bytes 8392704 | tf_op jit(solution)/shard_map/cond/branch_1_fun/gather | solution.py:68
  367.7 11.1 %fusion.57 = f32[2048,2048]{1,0:T(8,128)} fusion(f32[16,64,2048]{2,1,0:T(8,128)} %get-tuple-element.104, s32[2048]{0:T(1024)S(1)} %copy-done.10), kind=kOutput, calls=%fused_computation.101 | convolution fusion | flops 6442713088 | bytes 17833984 | tf_op jit(solution)/shard_map/cond/branch_1_fun/dot_general | solution.py:420
  378.8 15.9 %multiply_convert_fusion.1 = bf16[2048,1024]{1,0:T(8,128)(2,1)} fusion(f32[2048,2048]{1,0:T(8,128)} %gather_fusion.5, bf16[1024,2048]{1,0:T(8,128)(2,1)} %gather_fusion.6), kind=kOutput, calls=%fused_computation.82 | convolution fusion | flops 8604614656 | bytes 25165824 | tf_op jit(solution)/shard_map/cond/branch_1_fun/dot_general | solution.py:33
  394.7 15.4 %fusion.124 = f32[2048,2048]{1,0:T(8,128)} fusion(bf16[2048,1024]{1,0:T(8,128)(2,1)} %multiply_convert_fusion.1, bf16[1024,2048]{1,0:T(8,128)(2,1)} %gather_fusion.6), kind=kOutput, calls=%fused_computation.275 | convolution fusion | flops 8589934592 | bytes 25165824 | tf_op jit(solution)/shard_map/cond/branch_1_fun/dot_general | solution.py:33
  410.2 13.1 %fusion.46 = f32[1024,2048]{1,0:T(8,128)} fusion(bf16[2048,1024]{1,0:T(8,128)(2,1)} %multiply_convert_fusion.1, f32[2048,2048]{1,0:T(8,128)S(1)} %bitcast.65), kind=kOutput, calls=%fused_computation.89 | convolution fusion | flops 8594128896 | bytes 29360128 | tf_op jit(solution)/shard_map/cond/branch_1_fun/dot_general | solution.py:33
  423.3 6.8 fusion.50
  430.1 7.3 pad.14
  437.4 58.1 %all-to-all-done = f32[16,104,2048]{2,1,0:T(8,128)} async-done(((f32[16,104,2048]{2,1,0:T(8,128)}), f32[16,104,2048]{2,1,0:T(8,128)}, u32[]{:S(2)}, u32[]{:S(2)}) %all-to-all-start) | async-done | bytes 13631520 | tf_op jit(solution)/shard_map/cond/branch_1_fun/all_to_all | solution.py:64
  495.5 21.4 %gather_fusion.7 = f32[2048,2048]{1,0:T(8,128)} fusion(f32[1664,2048]{1,0:T(8,128)} %bitcast.16, s32[2048]{0:T(1024)S(1)} %get-tuple-element.156), kind=kCustom, calls=%fused_computation.7 | custom fusion | bytes 33562624 | tf_op jit(solution)/shard_map/cond/branch_1_fun/gather | solution.py:68
  516.9 16.5 %multiply_reduce_fusion.1 = f32[2048]{0:T(1024)S(1)} fusion(f32[2048,2048]{1,0:T(8,128)} %gather_fusion.5, f32[2048,2048]{1,0:T(8,128)} %fusion.57, f32[2048,2048]{1,0:T(8,128)} %gather_fusion.7, pred[2048]{0:T(1024)(128)(4,1)S(1)} %broadcast_compare_fusion.1), kind=kLoop, calls=%fused_computation.79 | loop fusion | flops 12580864 | bytes 50341888 | tf_op jit(solution)/shard_map/cond/branch_1_fun/reduce_sum | solution.py:454
  533.4 39.4 %scatter_custom_fusion.4 = f32[1792,2048]{1,0:T(8,128)} fusion(f32[1792,2048]{1,0:T(8,128)} %bitcast.71, s32[2048]{0:T(1024)} %get-tuple-element.157, f32[2048,2048]{1,0:T(8,128)} %gather_fusion.5, f32[2048]{0:T(1024)S(1)} %divide_add_fusion.1), kind=kCustom, calls=%fused_computation.72 | custom fusion | flops 12582912 | bytes 31465472 | tf_op jit(solution)/shard_map/cond/branch_1_fun/scatter-add | solution.py:426
  572.8 4.6 all-to-all-start.2
  577.4 39.0 %scatter_custom_fusion.3 = f32[1792,2048]{1,0:T(8,128)} fusion(s32[2048]{0:T(1024)} %get-tuple-element.163, f32[2048,2048]{1,0:T(8,128)} %fusion.124, f32[2048]{0:T(1024)S(1)} %divide_add_fusion.1, f32[]{:T(128)} %constant.298.clone, f32[2048,2048]{1,0:T(8,128)} %fusion.57, f32[2048,2048]{1,0:T(8,128)} %gather_fusion.7, ...), kind=kCustom, calls=%fused_computation.75 | custom fusion | flops 20971520 | bytes 65022464 | tf_op jit(solution)/shard_map/cond/branch_1_fun/scatter-add | solution.py:426
  616.4 136.6 %all-to-all-done.2.refs_5_ = f32[16,112,2048]{2,1,0:T(8,128)} async-done(((f32[16,112,2048]{2,1,0:T(8,128)}), f32[16,112,2048]{2,1,0:T(8,128)}, u32[]{:S(2)}, u32[]{:S(2)}) %all-to-all-start.2) | async-done | bytes 14680096 | tf_op jit(solution)/shard_map/cond/branch_1_fun/all_to_all | solution.py:64
  753.0 4.3 all-to-all-start.1
  757.3 18.7 %scatter_custom_fusion.5 = f32[896,2048]{1,0:T(8,128)} fusion(s32[1024]{0:T(1024)} %get-tuple-element.158, f32[1024,2048]{1,0:T(8,128)} %fusion.46, f32[]{:T(128)} %constant.298.clone), kind=kCustom, calls=%fused_computation.84 | custom fusion | flops 4194304 | bytes 15729152 | tf_op jit(solution)/shard_map/cond/branch_1_fun/scatter-add | solution.py:426
  776.0 156.9 %all-to-all-done.1.refs_3_ = f32[16,112,2048]{2,1,0:T(8,128)} async-done(((f32[16,112,2048]{2,1,0:T(8,128)}), f32[16,112,2048]{2,1,0:T(8,128)}, u32[]{:S(2)}, u32[]{:S(2)}) %all-to-all-start.1) | async-done | bytes 14680096 | tf_op jit(solution)/shard_map/cond/branch_1_fun/all_to_all | solution.py:64
  933.0 4.1 all-to-all-start.3
  942.1 93.3 %collect_lent.3 = f32[16,16,2048]{2,1,0:T(8,128)} custom-call(f32[16,2048]{1,0:T(8,128)} %pad_maximum_fusion.1.mine), custom_call_target="tpu_custom_call" | custom-call | tf_op jit(solution)/shard_map/cond/branch_1_fun/collect_lent/pallas_call | solution.py:297
  1035.3 1.3 slice_bitcast_fusion.1.refs_1_
  1036.7 39.3 %apply_rows.7 = f32[2000,2048]{1,0:T(8,128)} custom-call(s32[896]{0:T(1024)S(1)} %reshape.210.refs_0_, s32[1792]{0:T(1024)S(1)} %reshape.211.refs_1_, f32[8,2048]{1,0:T(8,128)S(1)} %broadcast_87_refs_2_.0.refs_2_, f32[2000,2048]{1,0:T(8,128)} %get-tuple-element.127.out_shard.refs_3_, f32[16,56,2048]{2,1,0:T(8,128)} %all-to-all-done.3.refs_4_, ...), custom_call_target="tpu_custom_call" | custom-call | flops 547880960 | bytes 54788096 | tf_op jit(solution)/shard_map/cond/branch_1_fun/apply_rows/pallas_call | solution.py:383
  1076.0 2.3 fusion.56
  1078.3 27.5 %apply_rows.6 = f32[2000,2048]{1,0:T(8,128)} custom-call(s32[1792]{0:T(1024)S(1)} %reshape.198.refs_0_, f32[128,2048]{1,0:T(8,128)S(1)} %slice_bitcast_fusion.1.refs_1_, f32[2000,2048]{1,0:T(8,128)} %get-tuple-element.129.in_shard.refs_2_, f32[16,112,2048]{2,1,0:T(8,128)} %all-to-all-done.1.refs_3_), custom_call_target="tpu_custom_call" | custom-call | flops 474480640 | bytes 47448064 | tf_op jit(solution)/shard_map/cond/branch_1_fun/apply_rows/pallas_call | solution.py:383
  (91 shorter events, 18.7 us)
Async XLA Ops:
  40.0 0.9 copy-start.8
  40.0 292.5 %copy-start.13 = (s32[2048]{0:T(1024)}, s32[2048]{0:T(1024)S(1)}, u32[]{:S(2)}) copy-start(s32[2048]{0:T(1024)S(1)} %get-tuple-element.102) | copy-start | bytes 24580 | tf_op jit(solution)/shard_map/cond
  55.4 3.1 copy-start.2
  328.7 166.8 %all-to-all-start = ((f32[16,104,2048]{2,1,0:T(8,128)}), f32[16,104,2048]{2,1,0:T(8,128)}, u32[]{:S(2)}, u32[]{:S(2)}) async-start(f32[16,104,2048]{2,1,0:T(8,128)} %get-tuple-element.108), calls=%async_computation | async-start | bytes 27262976 | tf_op jit(solution)/shard_map/cond/branch_1_fun/all_to_all | solution.py:64
  355.5 12.2 %copy-start.10 = (s32[2048]{0:T(1024)S(1)}, s32[2048]{0:T(1024)}, u32[]{:S(2)}) copy-start(s32[2048]{0:T(1024)} %get-tuple-element.103) | copy-start | bytes 24580 | tf_op jit(solution)/shard_map/cond
  378.8 31.4 %slice-start = ((s8[16777216]{0:T(1024)(128)(4,1)}), s8[4194304]{0:T(1024)(128)(4,1)S(1)}, s32[]{:S(2)}) async-start(s8[16777216]{0:T(1024)(128)(4,1)} %bitcast.64), calls=%async_computation.4 | async-start | bytes 8388608 | tf_op jit(solution)/shard_map/cond
  378.8 31.4 %slice-start.1 = ((s8[16777216]{0:T(1024)(128)(4,1)}), s8[4194304]{0:T(1024)(128)(4,1)S(1)}, s32[]{:S(2)}) async-start(s8[16777216]{0:T(1024)(128)(4,1)} %bitcast.64), calls=%async_computation.5 | async-start | bytes 8388608 | tf_op jit(solution)/shard_map/cond
  378.8 31.4 %slice-start.2 = ((s8[16777216]{0:T(1024)(128)(4,1)}), s8[4194304]{0:T(1024)(128)(4,1)S(1)}, s32[]{:S(2)}) async-start(s8[16777216]{0:T(1024)(128)(4,1)} %bitcast.64), calls=%async_computation.6 | async-start | bytes 8388608 | tf_op jit(solution)/shard_map/cond
  394.7 15.5 %slice-start.3 = ((s8[16777216]{0:T(1024)(128)(4,1)}), s8[4194304]{0:T(1024)(128)(4,1)S(1)}, s32[]{:S(2)}) async-start(s8[16777216]{0:T(1024)(128)(4,1)} %bitcast.64), calls=%async_computation.7 | async-start | bytes 8388608 | tf_op jit(solution)/shard_map/cond
  410.2 13.1 %copy-start.16 = (s32[1024]{0:T(1024)S(1)}, s32[1024]{0:T(1024)}, u32[]{:S(2)}) copy-start(s32[1024]{0:T(1024)} %get-tuple-element.111) | copy-start | bytes 12292 | tf_op jit(solution)/shard_map/cond
  423.3 14.1 %copy-start.14 = (s32[2048]{0:T(1024)S(1)}, s32[2048]{0:T(1024)}, u32[]{:S(2)}) copy-start(s32[2048]{0:T(1024)} %copy-done.13) | copy-start | bytes 24580 | tf_op jit(solution)/shard_map/cond
  572.8 180.2 %all-to-all-start.2 = ((f32[16,112,2048]{2,1,0:T(8,128)}), f32[16,112,2048]{2,1,0:T(8,128)}, u32[]{:S(2)}, u32[]{:S(2)}) async-start(f32[16,112,2048]{2,1,0:T(8,128)} %bitcast.72), calls=%async_computation.2 | async-start | bytes 29360128 | tf_op jit(solution)/shard_map/cond/branch_1_fun/all_to_all | solution.py:64
  753.0 180.0 %all-to-all-start.1 = ((f32[16,112,2048]{2,1,0:T(8,128)}), f32[16,112,2048]{2,1,0:T(8,128)}, u32[]{:S(2)}, u32[]{:S(2)}) async-start(f32[16,112,2048]{2,1,0:T(8,128)} %bitcast.73), calls=%async_computation.1 | async-start | bytes 29360128 | tf_op jit(solution)/shard_map/cond/branch_1_fun/all_to_all | solution.py:64
  757.3 179.7 %copy-start.17 = (s32[16,56]{1,0:T(8,128)S(1)}, s32[16,56]{1,0:T(8,128)}, u32[]{:S(2)}) copy-start(s32[16,56]{1,0:T(8,128)} %get-tuple-element.154) | copy-start | bytes 10756 | tf_op jit(solution)/shard_map/cond
  933.0 103.7 %all-to-all-start.3 = ((f32[16,56,2048]{2,1,0:T(8,128)}), f32[16,56,2048]{2,1,0:T(8,128)}, u32[]{:S(2)}, u32[]{:S(2)}) async-start(f32[16,56,2048]{2,1,0:T(8,128)} %bitcast.75), calls=%async_computation.3 | async-start | bytes 14680064 | tf_op jit(solution)/shard_map/cond/branch_1_fun/all_to_all | solution.py:64
  1036.7 39.3 %copy-start.4 = (f32[16,16,2048]{2,1,0:T(8,128)S(1)}, f32[16,16,2048]{2,1,0:T(8,128)}, u32[]{:S(2)}) copy-start(f32[16,16,2048]{2,1,0:T(8,128)} %collect_lent.3) | copy-start | bytes 6291460 | tf_op jit(solution)/shard_map/cond
